TPU v7x, 256 devices: a whole 4x4x8 slice. The times are simulated.
256 devices in a mesh: dp: 64 (over x, z, core), tensor: 4 (over y).
Axes of the slice: x: 4, y: 4, z: 8, core: 2. Of those that a mesh axis runs over, the one named last changes fastest.
Arguments:
- attn_out: bfloat16 [32768, 2560], P('dp', 'tensor'), may hold values from -6 to 6
- resid: bfloat16 [32768, 5120], P('dp', 'tensor'), may hold values from -6 to 6
- out_proj: bfloat16 [2560, 5120], P('tensor'), may hold values from -0.125 to 0.125
- heads: bfloat16 [5120, 8], P('tensor'), may hold values from -0.078125 to 0.078125
- gain: bfloat16 [5120], P('tensor'), may hold values from 0.25 to 1.75
- lengths: int32 [512], P('dp'), may hold values from 0 to 63
Outputs:
- uwo: float32 [512], P('dp')
- proj_grad: float32 [5120, 2560], P('dp', 'tensor')
- head_grad: float32 [5120, 8], P('tensor')
- gain_grad: float32 [5120], P('tensor')
Inputs may be any that keep to these rules, and one draw needn't show every extreme that they name: Positions 0 to lengths[n] of response n are scored.
All inputs are finite; a program needn't handle non-finite values.
Results may differ from a plain program's by a relative error of at most 0.0085.
Values may be sent and summed in bfloat16 or wider, within the bound.
No kernel may reach another device: no remote copies, remote signals or barrier semaphores. Data moves between devices by JAX's collectives and lax.ppermute only.
A program may use at most 128 MiB of HBM per device.

v0:
```python
import jax
import jax.numpy as jnp
from jax import lax
from jax.experimental import pallas as pl
from jax.experimental.pallas import tpu as pltpu
from jax.sharding import Mesh
from jax.sharding import PartitionSpec as P

D = 5120
SEQ = 64
EPS_NORM = 1e-06
EPS_VAR = 1e-05
PENALTY = 0.5
NX, NZ, NC, NY = 4, 8, 2, 4
LANES = 128
CUT = 256
ROWS = 256
MIB = 2**20
HI = lax.Precision.HIGHEST
BF = jnp.bfloat16
F32 = jnp.float32


together = lax.optimization_barrier


def exchanged(x, axis):
    return lax.all_to_all(x, axis, split_axis=0, concat_axis=0, tiled=True)


def shift(x, axis, by):
    n = lax.axis_size(axis)
    return lax.ppermute(x, axis, [(i, (i + by) % n) for i in range(n)])


def other_core(x):
    return lax.ppermute(x, "c", [(0, 1), (1, 0)])


def shift_by_core(x, axis):
    n = lax.axis_size(axis)
    moves = [(c, i, (i + 1 - 2 * c) % n) for c in range(NC) for i in range(n)]
    if axis == "y":
        return lax.ppermute(x, ("c", axis), [(c * n + i, c * n + j) for c, i, j in moves])
    return lax.ppermute(x, (axis, "c"), [(i * NC + c, j * NC + c) for c, i, j in moves])


def chunk_of(z, c):
    if c == 0:
        return 2 * z if z < NZ // 2 else 2 * (NZ - 1 - z) + 1
    return 2 * (z - NZ // 2) + 1 if z >= NZ // 2 else 2 * (NZ // 2 - 1 - z)


def final_places():
    pairs = []
    for x in range(NX):
        for z in range(NZ):
            for c in range(NC):
                for y in range(NY):
                    src = ((x * NZ + z) * NC + c) * NY + y
                    q = chunk_of(z, c)
                    dst = ((y * NZ + 4 * c + q // 2) * NC + q % 2) * NY + (y + x) % NY
                    pairs.append((src, dst))
    return pairs


def in_pieces(v, count):
    pieces = []
    for _ in range(count):
        high = lax.reduce_precision(v, 8, 7)
        pieces.append(high.astype(BF))
        v = v - high
    return pieces


def line_rows(line, count):
    return jnp.concatenate(in_pieces(line, count), axis=0)


def rows_line(rows, members):
    rows = rows.astype(F32)
    return sum(rows[i : i + members] for i in range(0, rows.shape[0], members))


def sum_rows(sums):
    small = jnp.concatenate(in_pieces(sums, 3), axis=1)
    return jnp.pad(small, ((0, 0), (0, LANES - small.shape[1])))


def rows_sum(rows):
    small = rows[:, :6].astype(F32)
    return small[:, 0:2] + small[:, 2:4] + small[:, 4:6]


def gathered_weight(out_proj, x, y, c):
    block = out_proj.shape[0]
    half = out_proj.shape[1] // (NY * NC)
    rows = block // NX
    picked = lax.dynamic_slice_in_dim(out_proj, x * rows, rows, 0)
    sent = jnp.stack(
        [lax.dynamic_slice_in_dim(picked, (2 * k + c) * half, half, 1) for k in range(NY)]
    )
    came = exchanged(sent, "y")
    own = jnp.stack(
        [lax.dynamic_index_in_dim(came, (y + r) % NY, 0, keepdims=False) for r in (1, 2, 3)]
    )
    low, high = shift(own, "x", 1), shift(own, "x", -1)
    low, high, onward = together((low, high, jnp.where(c == 0, low, high)))
    far = shift_by_core(onward, "x")
    return sent, (own, low, high, far)


def split(v):
    high = v.astype(BF)
    return high, (v - high.astype(F32)).astype(BF)


def dot(a, b):
    return jnp.dot(a, b, preferred_element_type=F32)


def hidden_kernel(where, *refs):
    rows, refs = refs[: NC * NY], refs[NC * NY :]
    out_proj, w_own, w_low, w_high, w_far, resid, pack, gh, hidden, sums, *refs = refs
    turned, a, w, res, sem = refs
    y, c, x = where[0], where[1], where[2]
    count, half = rows[0].shape
    part = w_own.shape[1]
    halves = (slice(0, count), slice(count, 2 * count))
    columns = lambda i: pl.ds(pl.multiple_of(i * half, LANES), half)
    copies = []

    def fetch(src, dst):
        copies.append(pltpu.make_async_copy(src, dst, sem.at[len(copies)]))
        copies[-1].start()
        return copies[-1]

    ready = [fetch(out_proj.at[:, columns(2 * y + c)], w.at[0])]
    for piece, owner in ((w_own, x), (w_low, x + NX - 1), (w_high, x + 1), (w_far, x + 2)):
        at = pl.ds(pl.multiple_of(lax.rem(owner, NX) * part, part), part)
        ready.append(fetch(piece, w.at[1:NY, at, :]))
    for i, r in enumerate((resid.at[:, columns(c)], pack.at[halves[0], :])):
        ready.append(fetch(r, res.at[halves[i], :]))
        for k in range(NY):
            ready.append(fetch(rows[NC * k + i], a.at[halves[i], k * half : (k + 1) * half]))
    early = len(ready) - NY - 1
    blocks = count // ROWS
    g_high, g_low = split(gh[...])
    lane = lax.broadcasted_iota(jnp.int32, (ROWS, LANES), 1)
    members = sums.shape[0] // 2

    def multiply(base):
        @pl.loop(0, blocks)
        def _(i):
            here = pl.ds(pl.multiple_of(base + i * ROWS, ROWS), ROWS)
            acc = res[here, :].astype(F32) + dot(a[here, :], w[...].reshape(NY * half, half))
            hidden[here, :] = acc
            high, low = split(acc)
            tile = dot(high, g_high) + dot(high, g_low) + dot(low, g_high)
            squares = jnp.sum(acc * acc, axis=1, keepdims=True)
            tile = jnp.where(lane == members, squares, tile).T
            sums[:, here] = tile[: 2 * members]

    for copy in ready[:early]:
        copy.wait()
    multiply(0)
    for copy in ready[early:]:
        copy.wait()
    moved = [
        fetch(a.at[:, columns(lax.rem(x + s, NX))], turned.at[s * NC * count : (s + 1) * NC * count])
        for s in range(NX)
    ]
    multiply(count)
    for copy in moved:
        copy.wait()


def hidden_and_sums(where, rows, out_proj, weights, resid, pack, gh):
    count, half = rows[0].shape
    members = gh.shape[1]
    total = NC * count
    gh = jnp.pad(gh, ((0, 0), (0, LANES - members)))
    any_space = pl.BlockSpec(memory_space=pl.ANY)
    full = lambda shape: pl.BlockSpec(shape, lambda i, s: (0, 0))
    return pl.pallas_call(
        hidden_kernel,
        grid_spec=pltpu.PrefetchScalarGridSpec(
            num_scalar_prefetch=1,
            grid=(1,),
            in_specs=[any_space] * (NC * NY + 7) + [full(gh.shape)],
            out_specs=[full((total, half)), full((2 * members, total)), any_space],
            scratch_shapes=[
                pltpu.VMEM((total, NY * half), BF),
                pltpu.VMEM((NY, half, half), BF),
                pltpu.VMEM((total, half), BF),
                pltpu.SemaphoreType.DMA((NC * NY + 7 + NX,)),
            ],
        ),
        out_shape=[
            jax.ShapeDtypeStruct((total, half), F32),
            jax.ShapeDtypeStruct((2 * members, total), F32),
            jax.ShapeDtypeStruct((NX * total, half), BF),
        ],
        compiler_params=pltpu.CompilerParams(vmem_limit_bytes=40 * MIB),
        cost_estimate=pl.CostEstimate(
            flops=8 * total * half * half, bytes_accessed=20 * MIB, transcendentals=0
        ),
        name="hidden_and_sums",
    )(where, *rows, out_proj, *weights, resid, pack, gh)


def step(attn_out, resid, out_proj, heads, gain, lengths):
    x, c, y = (lax.axis_index(a) for a in ("x", "c", "y"))
    count, _ = attn_out.shape
    members = heads.shape[1]
    half = resid.shape[1] // NC
    resp_own = lengths.shape[0]
    first = c == 0

    def own_half(a, axis, which):
        return lax.dynamic_slice_in_dim(a, which * half, half, axis)

    sent, weights = gathered_weight(out_proj, x, y, c)
    attn = together((attn_out, sent))[0]
    before, after = shift(attn, "y", 1), shift(attn, "y", -1)
    before, after, onward, resid_other = together(
        (before, after, jnp.where(first, before, after), resid)
    )
    far = shift_by_core(onward, "y")
    rows = [b for a in (attn, after, far, before) for b in (a, other_core(a))]
    lens_rows = jnp.zeros((8, half), BF).at[0, :resp_own].set(lengths.astype(BF))
    pack = other_core(jnp.concatenate([own_half(resid_other, 1, 1 - c), lens_rows], axis=0))
    lens = jnp.concatenate([lengths, pack[count, :resp_own].astype(jnp.int32)])
    total_rows, resp = 2 * count, 2 * resp_own
    gain_heads = own_half(gain, 0, c).astype(F32)[:, None] * own_half(heads, 0, c).astype(F32)
    where = jnp.stack([y, c, x]).astype(jnp.int32)
    hidden, part, turned = hidden_and_sums(
        where, rows, out_proj, weights, resid, pack, gain_heads
    )
    other = other_core(part)
    part = part + jnp.concatenate([other[:, count:], other[:, :count]], axis=1)
    part = part + shift(part, "y", 1) + shift(part, "y", -1) + shift(part, "y", 2)
    raw, squares = part[:members], part[members]

    rinv = lax.rsqrt(squares / D + EPS_NORM)
    scores = raw * rinv[None]
    counts = (lens + 1).astype(F32)
    at = lax.broadcasted_iota(jnp.int32, (resp, total_rows), 1) - SEQ * lax.broadcasted_iota(
        jnp.int32, (resp, total_rows), 0
    )
    inside = ((at >= 0) & (at <= lens[:, None])).astype(F32)
    rewards = jnp.einsum("kr,nr->kn", scores, inside, precision=HI) / counts[None]
    odd = lax.broadcasted_iota(jnp.int32, rewards.shape, 1) % 2 == 1
    partner = jnp.where(odd, jnp.roll(rewards, 1, 1), jnp.roll(rewards, -1, 1))
    sign = jnp.where(odd, 1.0, -1.0)
    dreward = sign * jax.nn.sigmoid(sign * (rewards - partner))
    dscore = jnp.einsum("kn,nr->kr", dreward / counts[None], inside, precision=HI)
    scaled = dscore * rinv[None]
    pull = rinv**3 * jnp.sum(dscore * raw, axis=0) / D
    dhidden = (
        jnp.einsum("kr,dk->rd", scaled, gain_heads, precision=HI) - hidden * pull[:, None]
    ).astype(BF)
    line = jnp.einsum("kr,rd->kd", scaled, hidden)
    sums = jnp.stack([jnp.sum(rewards, axis=1), jnp.sum(rewards * rewards, axis=1)], axis=1)

    near_a, up_a, far_a, down_a = (
        turned[s * total_rows : (s + 1) * total_rows] for s in range(NX)
    )

    def term(left, right):
        return jnp.einsum("rd,rj->dj", left, right, preferred_element_type=F32)

    slabs = (slice(CUT, None), slice(0, CUT))
    lines = [line[:, lanes] for lanes in slabs]
    extras = [sums, None]

    def with_rows(body, head, extra, count):
        rows = [body, line_rows(head, count)]
        if extra is not None:
            rows.append(jnp.pad(sum_rows(extra), ((0, 0), (0, body.shape[-1] - LANES))))
        return jnp.concatenate(rows, axis=0)

    def read_rows(rows, extra):
        if extra is None:
            return rows_line(rows, members), None
        return rows_line(rows[:-members], members), rows_sum(rows[-members:])

    came = []
    for lanes, head, extra in zip(slabs, lines, extras):
        outward = with_rows(term(dhidden, far_a[:, lanes]).astype(BF), head, extra, 2)
        outward, dhidden = together((outward, dhidden))
        came.append(shift_by_core(outward, "x"))
    near, up, down = together(tuple(term(dhidden, t) for t in (near_a, up_a, down_a)))

    sends = []
    for lanes, head, extra, got in zip(slabs, lines, extras, came):
        arrived = got[:half].astype(F32)
        got_head, got_extra = read_rows(got[half:], extra)

        def passed_on(t, use):
            body = (t[:, lanes] + jnp.where(use, arrived, 0.0)).astype(BF)
            more = None if extra is None else extra + jnp.where(use, got_extra, 0.0)
            return with_rows(body, head + jnp.where(use, got_head, 0.0), more, 2)

        pair = together((passed_on(up, first), passed_on(down, ~first)))
        got_up = shift(pair[0], "x", 1)
        got_down = shift(pair[1], "x", -1)
        sends.append((got_up, got_down))

    chunk = half // NZ
    totals = []
    for lanes, head, extra, (got_up, got_down) in zip(slabs, lines, extras, sends):
        body = near[:, lanes] + got_up[:half].astype(F32) + got_down[:half].astype(F32)
        up_head, up_extra = read_rows(got_up[half:], extra)
        down_head, down_extra = read_rows(got_down[half:], extra)
        head = head + up_head + down_head
        more = None if extra is None else extra + up_extra + down_extra
        totals.append(together((body.astype(BF), head, more)))

    body, head, extra = totals[0]
    rows = with_rows(body[:0], head, extra, 1)
    body = body.reshape(NZ, chunk, -1)
    orders = [jnp.stack([body[chunk_of(k, core)] for k in range(NZ)]) for core in range(NC)]
    blocks = jnp.concatenate(
        [jnp.where(first, *orders), jnp.broadcast_to(rows[None], (NZ, *rows.shape))], axis=1
    )
    done = exchanged(blocks, "z")
    done = done.astype(F32).sum(axis=0)
    head_0, reward_sums = read_rows(done[chunk:].astype(F32), extra)

    body, head, extra = totals[1]
    rows = line_rows(head, 1)

    def chunk_for(to):
        low = jnp.where(first, 2 * to, 2 * (NZ // 2 - 1 - to))
        high = jnp.where(first, 2 * (NZ - 1 - to) + 1, 2 * (to - NZ // 2) + 1)
        at = jnp.where(to < NZ // 2, low, high) * chunk
        return jnp.concatenate([lax.dynamic_slice_in_dim(body, at, chunk, 0), rows], axis=0)

    z = lax.axis_index("z")
    last = chunk_for(z).astype(F32)
    for s in (4, 3, 5, 2, 6, 1, 7):
        last = last + shift(chunk_for((z + s) % NZ), "z", s).astype(F32)
    proj = jnp.concatenate([last[:chunk], done[:chunk]], axis=1).astype(BF)
    proj = lax.ppermute(proj, ("x", "z", "c", "y"), final_places()).astype(F32)
    head_sum = jnp.concatenate([last[chunk:], head_0], axis=1)
    both = other_core(head_sum)
    whole_sum = jnp.concatenate(
        [jnp.where(first, head_sum, both), jnp.where(first, both, head_sum)], axis=1
    ).T
    head_grad = gain.astype(F32)[:, None] * whole_sum
    gain_grad = jnp.sum(heads.astype(F32) * whole_sum, axis=1)

    reward_sums = reward_sums / (resp * NX * NZ)
    center, second = reward_sums[:, 0], reward_sums[:, 1]
    spread = second - center * center
    zed = (rewards[:, :resp_own] - center[:, None]) * lax.rsqrt(spread + EPS_VAR)[:, None]
    zmean = jnp.mean(zed, axis=0)
    uwo = zmean - PENALTY * jnp.mean((zed - zmean[None]) ** 2, axis=0)
    return (uwo, proj, head_grad, gain_grad)


def solution(mesh):
    finer = Mesh(mesh.devices.reshape(NX, NZ, NC, NY), ("x", "z", "c", "y"))
    dp = ("x", "z", "c")
    in_specs = (P(dp, "y"), P(dp, "y"), P("y", None), P("y", None), P("y"), P(dp))
    out_specs = (P(dp), P(dp, "y"), P("y", None), P("y"))
    return jax.shard_map(step, mesh=finer, in_specs=in_specs, out_specs=out_specs, check_vma=False)
```

profile of v0, /device:TPU:17, one launch (start us, length us, event | category | flops | bytes accessed | tf_op | source)
XLA Modules:
  0.0 165.4 jit_solution(4913332885976010297)
XLA Ops:
  3.6 4.2 %all-to-all-start = ((bf16[4,160,640]{2,1,0:T(8,128)(2,1)}), bf16[4,160,640]{2,1,0:T(8,128)(2,1)S(1)}, u32[]{:S(2)}, u32[]{:S(2)}) async-start(bf16[4,160,640]{2,1,0:T(8,128)(2,1)} %pad_maximum_fusion), calls=%async_computation | async-start | bytes 1638400 | tf_op jit(solution)/shard_map/all_to_all | solution.py:28
  9.3 2.5 %collective-permute-start = (bf16[512,640]{1,0:T(8,128)(2,1)}, bf16[512,640]{1,0:T(8,128)(2,1)}, u32[]{:S(2)}, u32[]{:S(2)}) collective-permute-start(bf16[512,640]{1,0:T(8,128)(2,1)} %refs_0_), channel_id=1, source_target_pairs={{0,4},{4,0},{1,5},{5,1},{2,6},{6,2},{3,7},{7,3},{8,12},{12,8},{9,1... | collective-permute-start | bytes 1966088 | tf_op jit(solution)/shard_map/ppermute | solution.py:37
  11.8 4.4 %all-to-all-done = bf16[4,160,640]{2,1,0:T(8,128)(2,1)S(1)} async-done(((bf16[4,160,640]{2,1,0:T(8,128)(2,1)}), bf16[4,160,640]{2,1,0:T(8,128)(2,1)S(1)}, u32[]{:S(2)}, u32[]{:S(2)}) %all-to-all-start) | async-done | bytes 819232 | tf_op jit(solution)/shard_map/all_to_all | solution.py:28
  19.8 10.6 %collective-permute-done.1.refs_6_ = bf16[512,640]{1,0:T(8,128)(2,1)S(1)} collective-permute-done((bf16[512,640]{1,0:T(8,128)(2,1)}, bf16[512,640]{1,0:T(8,128)(2,1)S(1)}, u32[]{:S(2)}, u32[]{:S(2)}) %collective-permute-start.1) | collective-permute-done | bytes 655392 | tf_op jit(solution)/shard_map/ppermute | solution.py:33
  33.5 2.7 %collective-permute-start.10 = (bf16[520,640]{1,0:T(8,128)(2,1)}, bf16[520,640]{1,0:T(8,128)(2,1)}, u32[]{:S(2)}, u32[]{:S(2)}) collective-permute-start(bf16[520,640]{1,0:T(8,128)(2,1)} %fusion.15), channel_id=1, source_target_pairs={{0,4},{4,0},{1,5},{5,1},{2,6},{6,2},{3,7},{7,3},{8,12},{12,8},{9,1... | collective-permute-start | bytes 1996808 | tf_op jit(solution)/shard_map/ppermute | solution.py:37
  38.7 2.5 %collective-permute-start.9 = (bf16[3,160,640]{2,1,0:T(8,128)(2,1)}, bf16[3,160,640]{2,1,0:T(8,128)(2,1)}, u32[]{:S(2)}, u32[]{:S(2)}) collective-permute-start(bf16[3,160,640]{2,1,0:T(8,128)(2,1)} %broadcast_select_fusion.1), channel_id=1, source_target_pairs={{0,64},{64,128},{128,192},{192,0},{4,196},{68,4},{132,68},{196,132... | collective-permute-start | bytes 1843208 | tf_op jit(solution)/shard_map/ppermute | solution.py:45
  41.9 3.3 %collective-permute-start.5 = (bf16[512,640]{1,0:T(8,128)(2,1)}, bf16[512,640]{1,0:T(8,128)(2,1)}, u32[]{:S(2)}, u32[]{:S(2)}) collective-permute-start(bf16[512,640]{1,0:T(8,128)(2,1)} %collective-permute-done.4.refs_4_), channel_id=1, source_target_pairs={{0,4},{4,0},{1,5},{5,1},{2,6},{6,2},{3,7},{7,3},{8,12},{12,8},{9,1... | collective-permute-start | bytes 1966088 | tf_op jit(solution)/shard_map/ppermute | solution.py:37
  45.7 2.9 %collective-permute-done.9.refs_12_ = bf16[3,160,640]{2,1,0:T(8,128)(2,1)} collective-permute-done((bf16[3,160,640]{2,1,0:T(8,128)(2,1)}, bf16[3,160,640]{2,1,0:T(8,128)(2,1)}, u32[]{:S(2)}, u32[]{:S(2)}) %collective-permute-start.9) | collective-permute-done | bytes 614432 | tf_op jit(solution)/shard_map/ppermute | solution.py:45
  48.6 9.6 %hidden_and_sums.1 = (f32[1024,640]{1,0:T(8,128)S(1)}, f32[16,1024]{1,0:T(8,128)S(1)}, bf16[4096,640]{1,0:T(8,128)(2,1)}) custom-call(s32[3]{0:T(128)S(1)} %pad_add_fusion.where, bf16[512,640]{1,0:T(8,128)(2,1)} %refs_0_, bf16[512,640]{1,0:T(8,128)(2,1)} %collective-permute-done.refs_1_, bf16[512,640]{1,0:T(8,128)(2,1)S(1)} %collective-permute-done.2.refs_2_, ...), custom_call_target="tpu_custom_call" | custom-call | flops 3355443200 | bytes 20971520 | tf_op jit(solution)/shard_map/hidden_and_sums/pallas_call | solution.py:185
  69.0 3.0 %subtract_convert_fusion = bf16[1024,640]{1,0:T(8,128)(2,1)S(1)} fusion(f32[1024,640]{1,0:T(8,128)S(1)} %get-tuple-element.52, f32[1024]{0:T(1024)S(1)} %fusion.75, f32[8,1024]{1,0:T(8,128)S(1)} %get-tuple-element.162, f32[1024]{0:T(1024)S(1)} %bitcast.60, bf16[640,8]{1,0:T(8,128)(2,1)S(1)} %copy.22, f32[640]{0:T(1024)S(1)} %dynamic-slice_convert_fusion), kind=kOutput, calls=%fused_computation | convolution fusion | flops 64899072 | bytes 3985920 | tf_op jit(solution)/shard_map/kr,dk->rd/dot_general | solution.py:261
  76.1 2.5 %fusion.1 = f32[640,640]{1,0:T(8,128)S(1)} fusion(bf16[1024,640]{1,0:T(8,128)(2,1)S(1)} %subtract_convert_fusion, bf16[4096,640]{1,0:T(8,128)(2,1)} %get-tuple-element.53), kind=kOutput, calls=%fused_computation.3 | convolution fusion | flops 838860800 | bytes 4259840 | tf_op jit(solution)/shard_map/rd,rj->dj/dot_general | solution.py:271
  87.0 2.5 %collective-permute-start.20 = (bf16[656,256]{1,0:T(8,128)(2,1)}, bf16[656,256]{1,0:T(8,128)(2,1)}, u32[]{:S(2)}, u32[]{:S(2)}) collective-permute-start(bf16[656,256]{1,0:T(8,128)(2,1)} %pad_maximum_fusion.5), channel_id=1, source_target_pairs={{0,192},{64,0},{128,64},{192,128},{1,193},{65,1},{129,65},{193,129... | collective-permute-start | bytes 1007624 | tf_op jit(solution)/shard_map/ppermute | solution.py:33
  96.3 3.4 %collective-permute-done.19 = bf16[656,256]{1,0:T(8,128)(2,1)} collective-permute-done((bf16[656,256]{1,0:T(8,128)(2,1)}, bf16[656,256]{1,0:T(8,128)(2,1)}, u32[]{:S(2)}, u32[]{:S(2)}) %collective-permute-start.19) | collective-permute-done | bytes 335904 | tf_op jit(solution)/shard_map/ppermute | solution.py:33
  100.9 5.5 %collective-permute-done.17 = bf16[664,384]{1,0:T(8,128)(2,1)S(1)} collective-permute-done((bf16[664,384]{1,0:T(8,128)(2,1)S(1)}, bf16[664,384]{1,0:T(8,128)(2,1)S(1)}, u32[]{:S(2)}, u32[]{:S(2)}) %collective-permute-start.17) | collective-permute-done | bytes 509984 | tf_op jit(solution)/shard_map/ppermute | solution.py:33
  106.4 4.0 %collective-permute-done.16 = bf16[664,384]{1,0:T(8,128)(2,1)S(1)} collective-permute-done((bf16[664,384]{1,0:T(8,128)(2,1)S(1)}, bf16[664,384]{1,0:T(8,128)(2,1)S(1)}, u32[]{:S(2)}, u32[]{:S(2)}) %collective-permute-start.16) | collective-permute-done | bytes 509984 | tf_op jit(solution)/shard_map/ppermute | solution.py:33
  112.1 8.2 %all-to-all-start.1 = ((bf16[8,96,384]{2,1,0:T(8,128)(2,1)}), bf16[8,96,384]{2,1,0:T(8,128)(2,1)S(1)}, u32[]{:S(2)}, u32[]{:S(2)}) async-start(bf16[8,96,384]{2,1,0:T(8,128)(2,1)} %pad_maximum_fusion.2), calls=%async_computation.1 | async-start | bytes 1179648 | tf_op jit(solution)/shard_map/all_to_all | solution.py:28
  121.1 5.5 %collective-permute-start.21 = (bf16[88,256]{1,0:T(8,128)(2,1)S(1)}, bf16[88,256]{1,0:T(8,128)(2,1)S(1)}, u32[]{:S(2)}, u32[]{:S(2)}) collective-permute-start(bf16[88,256]{1,0:T(8,128)(2,1)S(1)} %get-tuple-element.139), channel_id=1, source_target_pairs={{0,32},{8,40},{16,48},{24,56},{32,0},{40,8},{48,16},{56,24},{1,33}... | collective-permute-start | bytes 135176 | tf_op jit(solution)/shard_map/ppermute | solution.py:33
  126.8 4.2 %collective-permute-start.23 = (bf16[88,256]{1,0:T(8,128)(2,1)S(1)}, bf16[88,256]{1,0:T(8,128)(2,1)S(1)}, u32[]{:S(2)}, u32[]{:S(2)}) collective-permute-start(bf16[88,256]{1,0:T(8,128)(2,1)S(1)} %get-tuple-element.141), channel_id=1, source_target_pairs={{0,40},{8,48},{16,56},{24,0},{32,8},{40,16},{48,24},{56,32},{1,41}... | collective-permute-start | bytes 135176 | tf_op jit(solution)/shard_map/ppermute | solution.py:33
  131.3 3.3 %collective-permute-start.25 = (bf16[88,256]{1,0:T(8,128)(2,1)S(1)}, bf16[88,256]{1,0:T(8,128)(2,1)S(1)}, u32[]{:S(2)}, u32[]{:S(2)}) collective-permute-start(bf16[88,256]{1,0:T(8,128)(2,1)S(1)} %get-tuple-element.143), channel_id=1, source_target_pairs={{0,48},{8,56},{16,0},{24,8},{32,16},{40,24},{48,32},{56,40},{1,49}... | collective-permute-start | bytes 135176 | tf_op jit(solution)/shard_map/ppermute | solution.py:33
  134.6 3.7 %collective-permute-done.21 = bf16[88,256]{1,0:T(8,128)(2,1)S(1)} collective-permute-done((bf16[88,256]{1,0:T(8,128)(2,1)S(1)}, bf16[88,256]{1,0:T(8,128)(2,1)S(1)}, u32[]{:S(2)}, u32[]{:S(2)}) %collective-permute-start.21) | collective-permute-done | bytes 45088 | tf_op jit(solution)/shard_map/ppermute | solution.py:33
  138.2 2.7 %collective-permute-start.27 = (bf16[88,256]{1,0:T(8,128)(2,1)S(1)}, bf16[88,256]{1,0:T(8,128)(2,1)S(1)}, u32[]{:S(2)}, u32[]{:S(2)}) collective-permute-start(bf16[88,256]{1,0:T(8,128)(2,1)S(1)} %get-tuple-element.145), channel_id=1, source_target_pairs={{0,56},{8,0},{16,8},{24,16},{32,24},{40,32},{48,40},{56,48},{1,57}... | collective-permute-start | bytes 135176 | tf_op jit(solution)/shard_map/ppermute | solution.py:33
  143.2 7.7 %collective-permute-start.29 = (f32[8,640]{1,0:T(8,128)S(1)}, f32[8,640]{1,0:T(8,128)S(1)}, u32[]{:S(2)}, u32[]{:S(2)}) collective-permute-start(f32[8,640]{1,0:T(8,128)S(1)} %pad_maximum_fusion.15), channel_id=1, source_target_pairs={{0,4},{4,0},{1,5},{5,1},{2,6},{6,2},{3,7},{7,3},{8,12},{12,8},{9,1... | collective-permute-start | bytes 61448 | tf_op jit(solution)/shard_map/ppermute | solution.py:37
  151.0 2.6 %collective-permute-start.28 = (bf16[80,640]{1,0:T(8,128)(2,1)S(1)}, bf16[80,640]{1,0:T(8,128)(2,1)S(1)}, u32[]{:S(2)}, u32[]{:S(2)}) collective-permute-start(bf16[80,640]{1,0:T(8,128)(2,1)S(1)} %pad_maximum_fusion.14), channel_id=1, source_target_pairs={{0,0},{1,65},{2,130},{3,195},{4,56},{5,121},{6,186},{7,251},{8,8},... | collective-permute-start | bytes 307208 | tf_op jit(solution)/shard_map/ppermute | solution.py:345
  155.7 9.0 %collective-permute-done.28 = bf16[80,640]{1,0:T(8,128)(2,1)S(1)} collective-permute-done((bf16[80,640]{1,0:T(8,128)(2,1)S(1)}, bf16[80,640]{1,0:T(8,128)(2,1)S(1)}, u32[]{:S(2)}, u32[]{:S(2)}) %collective-permute-start.28) | collective-permute-done | bytes 102432 | tf_op jit(solution)/shard_map/ppermute | solution.py:345
  (166 shorter events, 53.9 us)
Async XLA Ops:
  3.6 12.6 %all-to-all-start = ((bf16[4,160,640]{2,1,0:T(8,128)(2,1)}), bf16[4,160,640]{2,1,0:T(8,128)(2,1)S(1)}, u32[]{:S(2)}, u32[]{:S(2)}) async-start(bf16[4,160,640]{2,1,0:T(8,128)(2,1)} %pad_maximum_fusion), calls=%async_computation | async-start | bytes 1638400 | tf_op jit(solution)/shard_map/all_to_all | solution.py:28
  7.8 22.5 %collective-permute-start.1 = (bf16[512,640]{1,0:T(8,128)(2,1)}, bf16[512,640]{1,0:T(8,128)(2,1)S(1)}, u32[]{:S(2)}, u32[]{:S(2)}) collective-permute-start(bf16[512,640]{1,0:T(8,128)(2,1)} %refs_0_), channel_id=1, source_target_pairs={{0,1},{1,2},{2,3},{3,0},{4,5},{5,6},{6,7},{7,4},{8,9},{9,10},{10,1... | collective-permute-start | bytes 1966088 | tf_op jit(solution)/shard_map/ppermute | solution.py:33
  8.7 22.2 %collective-permute-start.2 = (bf16[512,640]{1,0:T(8,128)(2,1)}, bf16[512,640]{1,0:T(8,128)(2,1)S(1)}, u32[]{:S(2)}, u32[]{:S(2)}) collective-permute-start(bf16[512,640]{1,0:T(8,128)(2,1)} %refs_0_), channel_id=1, source_target_pairs={{0,3},{1,0},{2,1},{3,2},{4,7},{5,4},{6,5},{7,6},{8,11},{9,8},{10,9... | collective-permute-start | bytes 1966088 | tf_op jit(solution)/shard_map/ppermute | solution.py:33
  9.3 29.4 %collective-permute-start = (bf16[512,640]{1,0:T(8,128)(2,1)}, bf16[512,640]{1,0:T(8,128)(2,1)}, u32[]{:S(2)}, u32[]{:S(2)}) collective-permute-start(bf16[512,640]{1,0:T(8,128)(2,1)} %refs_0_), channel_id=1, source_target_pairs={{0,4},{4,0},{1,5},{5,1},{2,6},{6,2},{3,7},{7,3},{8,12},{12,8},{9,1... | collective-permute-start | bytes 1966088 | tf_op jit(solution)/shard_map/ppermute | solution.py:37
  16.4 19.8 %collective-permute-start.7 = (bf16[3,160,640]{2,1,0:T(8,128)(2,1)S(1)}, bf16[3,160,640]{2,1,0:T(8,128)(2,1)}, u32[]{:S(2)}, u32[]{:S(2)}) collective-permute-start(bf16[3,160,640]{2,1,0:T(8,128)(2,1)S(1)} %pad_maximum_fusion.1.refs_9_), channel_id=1, source_target_pairs={{0,64},{64,128},{128,192},{192,0},{1,65},{65,129},{129,193},{193,1... | collective-permute-start | bytes 1843208 | tf_op jit(solution)/shard_map/ppermute | solution.py:33
  18.4 17.8 %collective-permute-start.8 = (bf16[3,160,640]{2,1,0:T(8,128)(2,1)S(1)}, bf16[3,160,640]{2,1,0:T(8,128)(2,1)}, u32[]{:S(2)}, u32[]{:S(2)}) collective-permute-start(bf16[3,160,640]{2,1,0:T(8,128)(2,1)S(1)} %pad_maximum_fusion.1.refs_9_), channel_id=1, source_target_pairs={{0,192},{64,0},{128,64},{192,128},{1,193},{65,1},{129,65},{193,129... | collective-permute-start | bytes 1843208 | tf_op jit(solution)/shard_map/ppermute | solution.py:33
  31.8 10.0 %collective-permute-start.4 = (bf16[512,640]{1,0:T(8,128)(2,1)}, bf16[512,640]{1,0:T(8,128)(2,1)}, u32[]{:S(2)}, u32[]{:S(2)}) collective-permute-start(bf16[512,640]{1,0:T(8,128)(2,1)} %broadcast_select_fusion), channel_id=1, source_target_pairs={{0,1},{1,2},{2,3},{3,0},{4,7},{5,4},{6,5},{7,6},{8,9},{9,10},{10,1... | collective-permute-start | bytes 1966088 | tf_op jit(solution)/shard_map/ppermute | solution.py:44
  33.5 12.3 %collective-permute-start.10 = (bf16[520,640]{1,0:T(8,128)(2,1)}, bf16[520,640]{1,0:T(8,128)(2,1)}, u32[]{:S(2)}, u32[]{:S(2)}) collective-permute-start(bf16[520,640]{1,0:T(8,128)(2,1)} %fusion.15), channel_id=1, source_target_pairs={{0,4},{4,0},{1,5},{5,1},{2,6},{6,2},{3,7},{7,3},{8,12},{12,8},{9,1... | collective-permute-start | bytes 1996808 | tf_op jit(solution)/shard_map/ppermute | solution.py:37
  36.2 9.5 %collective-permute-start.3 = (bf16[512,640]{1,0:T(8,128)(2,1)S(1)}, bf16[512,640]{1,0:T(8,128)(2,1)}, u32[]{:S(2)}, u32[]{:S(2)}) collective-permute-start(bf16[512,640]{1,0:T(8,128)(2,1)S(1)} %collective-permute-done.2.refs_2_), channel_id=1, source_target_pairs={{0,4},{4,0},{1,5},{5,1},{2,6},{6,2},{3,7},{7,3},{8,12},{12,8},{9,1... | collective-permute-start | bytes 1966088 | tf_op jit(solution)/shard_map/ppermute | solution.py:37
  36.2 9.5 %collective-permute-start.6 = (bf16[512,640]{1,0:T(8,128)(2,1)S(1)}, bf16[512,640]{1,0:T(8,128)(2,1)}, u32[]{:S(2)}, u32[]{:S(2)}) collective-permute-start(bf16[512,640]{1,0:T(8,128)(2,1)S(1)} %collective-permute-done.1.refs_6_), channel_id=1, source_target_pairs={{0,4},{4,0},{1,5},{5,1},{2,6},{6,2},{3,7},{7,3},{8,12},{12,8},{9,1... | collective-permute-start | bytes 1966088 | tf_op jit(solution)/shard_map/ppermute | solution.py:37
  38.7 9.9 %collective-permute-start.9 = (bf16[3,160,640]{2,1,0:T(8,128)(2,1)}, bf16[3,160,640]{2,1,0:T(8,128)(2,1)}, u32[]{:S(2)}, u32[]{:S(2)}) collective-permute-start(bf16[3,160,640]{2,1,0:T(8,128)(2,1)} %broadcast_select_fusion.1), channel_id=1, source_target_pairs={{0,64},{64,128},{128,192},{192,0},{4,196},{68,4},{132,68},{196,132... | collective-permute-start | bytes 1843208 | tf_op jit(solution)/shard_map/ppermute | solution.py:45
  83.0 8.2 %collective-permute-start.15 = (bf16[664,384]{1,0:T(8,128)(2,1)S(1)}, bf16[664,384]{1,0:T(8,128)(2,1)S(1)}, u32[]{:S(2)}, u32[]{:S(2)}) collective-permute-start(bf16[664,384]{1,0:T(8,128)(2,1)S(1)} %fusion.21), channel_id=1, source_target_pairs={{0,64},{64,128},{128,192},{192,0},{4,196},{68,4},{132,68},{196,132... | collective-permute-start | bytes 1529864 | tf_op jit(solution)/shard_map/ppermute | solution.py:45
  87.0 8.6 %collective-permute-start.20 = (bf16[656,256]{1,0:T(8,128)(2,1)}, bf16[656,256]{1,0:T(8,128)(2,1)}, u32[]{:S(2)}, u32[]{:S(2)}) collective-permute-start(bf16[656,256]{1,0:T(8,128)(2,1)} %pad_maximum_fusion.5), channel_id=1, source_target_pairs={{0,192},{64,0},{128,64},{192,128},{1,193},{65,1},{129,65},{193,129... | collective-permute-start | bytes 1007624 | tf_op jit(solution)/shard_map/ppermute | solution.py:33
  89.5 10.3 %collective-permute-start.19 = (bf16[656,256]{1,0:T(8,128)(2,1)}, bf16[656,256]{1,0:T(8,128)(2,1)}, u32[]{:S(2)}, u32[]{:S(2)}) collective-permute-start(bf16[656,256]{1,0:T(8,128)(2,1)} %pad_maximum_fusion.4), channel_id=1, source_target_pairs={{0,64},{64,128},{128,192},{192,0},{1,65},{65,129},{129,193},{193,1... | collective-permute-start | bytes 1007624 | tf_op jit(solution)/shard_map/ppermute | solution.py:33
  91.9 14.5 %collective-permute-start.17 = (bf16[664,384]{1,0:T(8,128)(2,1)S(1)}, bf16[664,384]{1,0:T(8,128)(2,1)S(1)}, u32[]{:S(2)}, u32[]{:S(2)}) collective-permute-start(bf16[664,384]{1,0:T(8,128)(2,1)S(1)} %fusion.23), channel_id=1, source_target_pairs={{0,192},{64,0},{128,64},{192,128},{1,193},{65,1},{129,65},{193,129... | collective-permute-start | bytes 1529864 | tf_op jit(solution)/shard_map/ppermute | solution.py:33
  93.9 16.5 %collective-permute-start.16 = (bf16[664,384]{1,0:T(8,128)(2,1)S(1)}, bf16[664,384]{1,0:T(8,128)(2,1)S(1)}, u32[]{:S(2)}, u32[]{:S(2)}) collective-permute-start(bf16[664,384]{1,0:T(8,128)(2,1)S(1)} %fusion.22), channel_id=1, source_target_pairs={{0,64},{64,128},{128,192},{192,0},{1,65},{65,129},{129,193},{193,1... | collective-permute-start | bytes 1529864 | tf_op jit(solution)/shard_map/ppermute | solution.py:33
  112.1 31.0 %all-to-all-start.1 = ((bf16[8,96,384]{2,1,0:T(8,128)(2,1)}), bf16[8,96,384]{2,1,0:T(8,128)(2,1)S(1)}, u32[]{:S(2)}, u32[]{:S(2)}) async-start(bf16[8,96,384]{2,1,0:T(8,128)(2,1)} %pad_maximum_fusion.2), calls=%async_computation.1 | async-start | bytes 1179648 | tf_op jit(solution)/shard_map/all_to_all | solution.py:28
  121.1 17.2 %collective-permute-start.21 = (bf16[88,256]{1,0:T(8,128)(2,1)S(1)}, bf16[88,256]{1,0:T(8,128)(2,1)S(1)}, u32[]{:S(2)}, u32[]{:S(2)}) collective-permute-start(bf16[88,256]{1,0:T(8,128)(2,1)S(1)} %get-tuple-element.139), channel_id=1, source_target_pairs={{0,32},{8,40},{16,48},{24,56},{32,0},{40,8},{48,16},{56,24},{1,33}... | collective-permute-start | bytes 135176 | tf_op jit(solution)/shard_map/ppermute | solution.py:33
  126.5 11.7 %collective-permute-start.22 = (bf16[88,256]{1,0:T(8,128)(2,1)S(1)}, bf16[88,256]{1,0:T(8,128)(2,1)S(1)}, u32[]{:S(2)}, u32[]{:S(2)}) collective-permute-start(bf16[88,256]{1,0:T(8,128)(2,1)S(1)} %get-tuple-element.140), channel_id=1, source_target_pairs={{0,24},{8,32},{16,40},{24,48},{32,56},{40,0},{48,8},{56,16},{1,25}... | collective-permute-start | bytes 135176 | tf_op jit(solution)/shard_map/ppermute | solution.py:33
  126.8 14.1 %collective-permute-start.23 = (bf16[88,256]{1,0:T(8,128)(2,1)S(1)}, bf16[88,256]{1,0:T(8,128)(2,1)S(1)}, u32[]{:S(2)}, u32[]{:S(2)}) collective-permute-start(bf16[88,256]{1,0:T(8,128)(2,1)S(1)} %get-tuple-element.141), channel_id=1, source_target_pairs={{0,40},{8,48},{16,56},{24,0},{32,8},{40,16},{48,24},{56,32},{1,41}... | collective-permute-start | bytes 135176 | tf_op jit(solution)/shard_map/ppermute | solution.py:33
  131.0 10.4 %collective-permute-start.24 = (bf16[88,256]{1,0:T(8,128)(2,1)S(1)}, bf16[88,256]{1,0:T(8,128)(2,1)S(1)}, u32[]{:S(2)}, u32[]{:S(2)}) collective-permute-start(bf16[88,256]{1,0:T(8,128)(2,1)S(1)} %get-tuple-element.142), channel_id=1, source_target_pairs={{0,16},{8,24},{16,32},{24,40},{32,48},{40,56},{48,0},{56,8},{1,17}... | collective-permute-start | bytes 135176 | tf_op jit(solution)/shard_map/ppermute | solution.py:33
  131.3 10.2 %collective-permute-start.25 = (bf16[88,256]{1,0:T(8,128)(2,1)S(1)}, bf16[88,256]{1,0:T(8,128)(2,1)S(1)}, u32[]{:S(2)}, u32[]{:S(2)}) collective-permute-start(bf16[88,256]{1,0:T(8,128)(2,1)S(1)} %get-tuple-element.143), channel_id=1, source_target_pairs={{0,48},{8,56},{16,0},{24,8},{32,16},{40,24},{48,32},{56,40},{1,49}... | collective-permute-start | bytes 135176 | tf_op jit(solution)/shard_map/ppermute | solution.py:33
  143.2 11.2 %collective-permute-start.29 = (f32[8,640]{1,0:T(8,128)S(1)}, f32[8,640]{1,0:T(8,128)S(1)}, u32[]{:S(2)}, u32[]{:S(2)}) collective-permute-start(f32[8,640]{1,0:T(8,128)S(1)} %pad_maximum_fusion.15), channel_id=1, source_target_pairs={{0,4},{4,0},{1,5},{5,1},{2,6},{6,2},{3,7},{7,3},{8,12},{12,8},{9,1... | collective-permute-start | bytes 61448 | tf_op jit(solution)/shard_map/ppermute | solution.py:37
  151.0 13.7 %collective-permute-start.28 = (bf16[80,640]{1,0:T(8,128)(2,1)S(1)}, bf16[80,640]{1,0:T(8,128)(2,1)S(1)}, u32[]{:S(2)}, u32[]{:S(2)}) collective-permute-start(bf16[80,640]{1,0:T(8,128)(2,1)S(1)} %pad_maximum_fusion.14), channel_id=1, source_target_pairs={{0,0},{1,65},{2,130},{3,195},{4,56},{5,121},{6,186},{7,251},{8,8},... | collective-permute-start | bytes 307208 | tf_op jit(solution)/shard_map/ppermute | solution.py:345
  (15 other events, 147.6 us)
where the time goes:
time: 166 us; the launch traced here: 165 us
  starting transfers between devices  68.6 us (41%)
  waiting for transfers between devices  55 us (33%)
  other arithmetic  15.6 us (9%)
  matrix products  12.7 us (8%)
  Pallas kernels  9.6 us (6%)
  local copies, waits for them, and re-layouts  2.71 us (2%)
    ppermute x18, waiting for transfers between devices, shift(): return lax.ppermute(x, axis, [(i, (i + by) % n) for i in range(n)])  34.2 us
    ppermute x18, starting transfers between devices, shift(): return lax.ppermute(x, axis, [(i, (i + by) % n) for i in range(n)])  29.6 us
    ppermute x7, starting transfers between devices, other_core(): return lax.ppermute(x, 'c', [(0, 1), (1, 0)])  18.7 us
    all_to_all x2, starting transfers between devices, exchanged(): return lax.all_to_all(x, axis, split_axis=0, concat_axis=0, tiled=True)  12.4 us
    pallas_call x1, Pallas kernels, hidden_and_sums(): pl.pallas_call(hidden_kernel, grid_spec=pltpu.PrefetchScalarGridSpec(num_...  9.6 us
    ppermute x1, waiting for transfers between devices, step(): proj = lax.ppermute(proj, ('x', 'z', 'c', 'y'), final_places()).astype(F32)  8.96 us
    dot_general x5, matrix products, term(): return jnp.einsum('rd,rj->dj', left, right, preferred_element_type=F32)  8.87 us
    ppermute x3, waiting for transfers between devices, shift_by_core(): lax.ppermute(x, (axis, 'c'), [(i * NC + c, j * NC + c) for c, i, j in mov...  6.58 us
  transfers between devices with their start and end apart: 32, of which 18 were waited for; matrix products, arithmetic and copies ran while one was open for 9% of the time, Pallas kernels for 0%

commit v1 on v0

--- a/solution.py
+++ b/solution.py
@@ -13,7 +13,7 @@
 PENALTY = 0.5
 NX, NZ, NC, NY = 4, 8, 2, 4
 LANES = 128
-CUT = 256
+CUT = 384
 ROWS = 256
 MIB = 2**20
 HI = lax.Precision.HIGHEST
@@ -166,8 +166,9 @@
     multiply(0)
     for copy in ready[early:]:
         copy.wait()
+    whole = NC * count
     moved = [
-        fetch(a.at[:, columns(lax.rem(x + s, NX))], turned.at[s * NC * count : (s + 1) * NC * count])
+        fetch(a.at[:, columns(lax.rem(x + s, NX))], turned.at[s * whole : (s + 1) * whole])
         for s in range(NX)
     ]
     multiply(count)
@@ -193,7 +194,7 @@
                 pltpu.VMEM((total, NY * half), BF),
                 pltpu.VMEM((NY, half, half), BF),
                 pltpu.VMEM((total, half), BF),
-                pltpu.SemaphoreType.DMA((NC * NY + 7 + NX,)),
+                pltpu.SemaphoreType.DMA((24,)),
             ],
         ),
         out_shape=[
@@ -201,7 +202,7 @@
             jax.ShapeDtypeStruct((2 * members, total), F32),
             jax.ShapeDtypeStruct((NX * total, half), BF),
         ],
-        compiler_params=pltpu.CompilerParams(vmem_limit_bytes=40 * MIB),
+        compiler_params=pltpu.CompilerParams(vmem_limit_bytes=52 * MIB),
         cost_estimate=pl.CostEstimate(
             flops=8 * total * half * half, bytes_accessed=20 * MIB, transcendentals=0
         ),
@@ -211,7 +212,7 @@
 
 def step(attn_out, resid, out_proj, heads, gain, lengths):
     x, c, y = (lax.axis_index(a) for a in ("x", "c", "y"))
-    count, _ = attn_out.shape
+    count, block = attn_out.shape
     members = heads.shape[1]
     half = resid.shape[1] // NC
     resp_own = lengths.shape[0]
@@ -223,13 +224,11 @@
     sent, weights = gathered_weight(out_proj, x, y, c)
     attn = together((attn_out, sent))[0]
     before, after = shift(attn, "y", 1), shift(attn, "y", -1)
-    before, after, onward, resid_other = together(
-        (before, after, jnp.where(first, before, after), resid)
-    )
-    far = shift_by_core(onward, "y")
+    far = shift_by_core(jnp.where(first, before, after), "y")
     rows = [b for a in (attn, after, far, before) for b in (a, other_core(a))]
     lens_rows = jnp.zeros((8, half), BF).at[0, :resp_own].set(lengths.astype(BF))
-    pack = other_core(jnp.concatenate([own_half(resid_other, 1, 1 - c), lens_rows], axis=0))
+    pack = jnp.concatenate([own_half(resid, 1, 1 - c), lens_rows], axis=0)
+    pack = other_core(pack)
     lens = jnp.concatenate([lengths, pack[count, :resp_own].astype(jnp.int32)])
     total_rows, resp = 2 * count, 2 * resp_own
     gain_heads = own_half(gain, 0, c).astype(F32)[:, None] * own_half(heads, 0, c).astype(F32)
@@ -257,49 +256,60 @@
     dscore = jnp.einsum("kn,nr->kr", dreward / counts[None], inside, precision=HI)
     scaled = dscore * rinv[None]
     pull = rinv**3 * jnp.sum(dscore * raw, axis=0) / D
+    s_high, s_low = in_pieces(scaled, 2)
+    g_high, g_low = in_pieces(together((gain_heads.T, hidden))[0], 2)
+    left = jnp.concatenate([s_high, s_low, s_high], axis=0)
+    right = jnp.concatenate([g_high, g_high, g_low], axis=0)
     dhidden = (
-        jnp.einsum("kr,dk->rd", scaled, gain_heads, precision=HI) - hidden * pull[:, None]
+        jnp.einsum("kr,kd->rd", left, right, preferred_element_type=F32) - hidden * pull[:, None]
     ).astype(BF)
     line = jnp.einsum("kr,rd->kd", scaled, hidden)
     sums = jnp.stack([jnp.sum(rewards, axis=1), jnp.sum(rewards * rewards, axis=1)], axis=1)
 
     near_a, up_a, far_a, down_a = (
-        turned[s * total_rows : (s + 1) * total_rows] for s in range(NX)
-    )
+        turned[i * total_rows : (i + 1) * total_rows] for i in range(NX)
+    )
+    far_a = together(far_a)
 
     def term(left, right):
         return jnp.einsum("rd,rj->dj", left, right, preferred_element_type=F32)
 
     slabs = (slice(CUT, None), slice(0, CUT))
-    lines = [line[:, lanes] for lanes in slabs]
-    extras = [sums, None]
+    tiles = -(-block // CUT)
+    line = jnp.pad(line, ((0, 0), (0, tiles * CUT - block)))
+    line = jnp.concatenate([line[:, i * CUT : (i + 1) * CUT] for i in range(tiles)], axis=0)
+    tall = line.shape[0]
+    lines, extras = [None, line], [None, sums]
 
     def with_rows(body, head, extra, count):
-        rows = [body, line_rows(head, count)]
-        if extra is not None:
-            rows.append(jnp.pad(sum_rows(extra), ((0, 0), (0, body.shape[-1] - LANES))))
-        return jnp.concatenate(rows, axis=0)
-
-    def read_rows(rows, extra):
-        if extra is None:
-            return rows_line(rows, members), None
-        return rows_line(rows[:-members], members), rows_sum(rows[-members:])
+        if head is None:
+            return body
+        small = jnp.pad(sum_rows(extra), ((0, 0), (0, CUT - LANES)))
+        return jnp.concatenate([body, line_rows(head, count), small], axis=0)
+
+    def read_rows(rows, head):
+        if head is None:
+            return None, None
+        return rows_line(rows[:-members], tall), rows_sum(rows[-members:])
 
     came = []
     for lanes, head, extra in zip(slabs, lines, extras):
         outward = with_rows(term(dhidden, far_a[:, lanes]).astype(BF), head, extra, 2)
         outward, dhidden = together((outward, dhidden))
         came.append(shift_by_core(outward, "x"))
-    near, up, down = together(tuple(term(dhidden, t) for t in (near_a, up_a, down_a)))
+    up, down = together(tuple(term(dhidden, t) for t in (up_a, down_a)))
+    near = together(term(dhidden, near_a))
 
     sends = []
     for lanes, head, extra, got in zip(slabs, lines, extras, came):
         arrived = got[:half].astype(F32)
-        got_head, got_extra = read_rows(got[half:], extra)
+        got_head, got_extra = read_rows(got[half:], head)
 
         def passed_on(t, use):
             body = (t[:, lanes] + jnp.where(use, arrived, 0.0)).astype(BF)
-            more = None if extra is None else extra + jnp.where(use, got_extra, 0.0)
+            if head is None:
+                return body
+            more = extra + jnp.where(use, got_extra, 0.0)
             return with_rows(body, head + jnp.where(use, got_head, 0.0), more, 2)
 
         pair = together((passed_on(up, first), passed_on(down, ~first)))
@@ -311,25 +321,19 @@
     totals = []
     for lanes, head, extra, (got_up, got_down) in zip(slabs, lines, extras, sends):
         body = near[:, lanes] + got_up[:half].astype(F32) + got_down[:half].astype(F32)
-        up_head, up_extra = read_rows(got_up[half:], extra)
-        down_head, down_extra = read_rows(got_down[half:], extra)
-        head = head + up_head + down_head
-        more = None if extra is None else extra + up_extra + down_extra
-        totals.append(together((body.astype(BF), head, more)))
-
-    body, head, extra = totals[0]
+        if head is not None:
+            up_head, up_extra = read_rows(got_up[half:], head)
+            down_head, down_extra = read_rows(got_down[half:], head)
+            head, extra = head + up_head + down_head, extra + up_extra + down_extra
+        totals.append(together((body.astype(BF), head, extra)))
+
+    body = totals[0][0].reshape(NZ, chunk, -1)
+    orders = [jnp.stack([body[chunk_of(k, core)] for k in range(NZ)]) for core in range(NC)]
+    done = exchanged(jnp.where(first, *orders), "z")
+    done = done.astype(F32).sum(axis=0)
+
+    body, head, extra = totals[1]
     rows = with_rows(body[:0], head, extra, 1)
-    body = body.reshape(NZ, chunk, -1)
-    orders = [jnp.stack([body[chunk_of(k, core)] for k in range(NZ)]) for core in range(NC)]
-    blocks = jnp.concatenate(
-        [jnp.where(first, *orders), jnp.broadcast_to(rows[None], (NZ, *rows.shape))], axis=1
-    )
-    done = exchanged(blocks, "z")
-    done = done.astype(F32).sum(axis=0)
-    head_0, reward_sums = read_rows(done[chunk:].astype(F32), extra)
-
-    body, head, extra = totals[1]
-    rows = line_rows(head, 1)
 
     def chunk_for(to):
         low = jnp.where(first, 2 * to, 2 * (NZ // 2 - 1 - to))
@@ -341,9 +345,11 @@
     last = chunk_for(z).astype(F32)
     for s in (4, 3, 5, 2, 6, 1, 7):
         last = last + shift(chunk_for((z + s) % NZ), "z", s).astype(F32)
-    proj = jnp.concatenate([last[:chunk], done[:chunk]], axis=1).astype(BF)
+    proj = jnp.concatenate([last[:chunk], done], axis=1).astype(BF)
     proj = lax.ppermute(proj, ("x", "z", "c", "y"), final_places()).astype(F32)
-    head_sum = jnp.concatenate([last[chunk:], head_0], axis=1)
+    head_sum = last[chunk : chunk + tall]
+    head_sum = jnp.concatenate([head_sum[i : i + members] for i in range(0, tall, members)], axis=1)
+    head_sum, reward_sums = head_sum[:, :block], rows_sum(last[-members:])
     both = other_core(head_sum)
     whole_sum = jnp.concatenate(
         [jnp.where(first, head_sum, both), jnp.where(first, both, head_sum)], axis=1

time: 166 us -> 161 us (0.970)
  the two profiles are of different devices: /device:TPU:17 before, /device:TPU:6 now
where the time goes in v1:
time: 161 us
  waiting for transfers between devices  73.4 us (46%)
  starting transfers between devices  49.1 us (30%)
  Pallas kernels  11.3 us (7%)
  other arithmetic  10.6 us (7%)
  matrix products  10.6 us (7%)
  local copies, waits for them, and re-layouts  4.41 us (3%)
    ppermute x18, starting transfers between devices, shift(): return lax.ppermute(x, axis, [(i, (i + by) % n) for i in range(n)])  33.5 us
    ppermute x18, waiting for transfers between devices, shift(): return lax.ppermute(x, axis, [(i, (i + by) % n) for i in range(n)])  29.5 us
    all_to_all x2, waiting for transfers between devices, exchanged(): return lax.all_to_all(x, axis, split_axis=0, concat_axis=0, tiled=True)  18.6 us
    pallas_call x1, Pallas kernels, hidden_and_sums(): pl.pallas_call(hidden_kernel, grid_spec=pltpu.PrefetchScalarGridSpec(num_...  11.3 us
    ppermute x1, waiting for transfers between devices, shift_by_core(): lax.ppermute(x, ('c', axis), [(c * n + i, c * n + j) for c, i, j in moves])  9.15 us
    dot_general x5, matrix products, term(): return jnp.einsum('rd,rj->dj', left, right, preferred_element_type=F32)  9.07 us
    ppermute x3, waiting for transfers between devices, shift_by_core(): lax.ppermute(x, (axis, 'c'), [(i * NC + c, j * NC + c) for c, i, j in mov...  8.14 us
    all_to_all x2, starting transfers between devices, exchanged(): return lax.all_to_all(x, axis, split_axis=0, concat_axis=0, tiled=True)  8.03 us
  transfers between devices with their start and end apart: 32, of which 18 were waited for; matrix products, arithmetic and copies ran while one was open for 8% of the time, Pallas kernels for 0%

profile of v1, /device:TPU:6, one launch (start us, length us, event | category | flops | bytes accessed | tf_op | source)
XLA Modules:
  0.0 160.8 jit_solution(7050376105714787026)
XLA Ops:
  3.6 4.6 %all-to-all-start = ((bf16[4,160,640]{2,1,0:T(8,128)(2,1)}), bf16[4,160,640]{2,1,0:T(8,128)(2,1)S(1)}, u32[]{:S(2)}, u32[]{:S(2)}) async-start(bf16[4,160,640]{2,1,0:T(8,128)(2,1)} %pad_maximum_fusion), calls=%async_computation | async-start | bytes 1638400 | tf_op jit(solution)/shard_map/all_to_all | solution.py:28
  8.2 3.2 %collective-permute-start.1 = (bf16[512,640]{1,0:T(8,128)(2,1)}, bf16[512,640]{1,0:T(8,128)(2,1)S(1)}, u32[]{:S(2)}, u32[]{:S(2)}) collective-permute-start(bf16[512,640]{1,0:T(8,128)(2,1)} %refs_0_), channel_id=1, source_target_pairs={{0,3},{1,0},{2,1},{3,2},{4,7},{5,4},{6,5},{7,6},{8,11},{9,8},{10,9... | collective-permute-start | bytes 1966088 | tf_op jit(solution)/shard_map/ppermute | solution.py:33
  12.4 9.9 %all-to-all-done = bf16[4,160,640]{2,1,0:T(8,128)(2,1)S(1)} async-done(((bf16[4,160,640]{2,1,0:T(8,128)(2,1)}), bf16[4,160,640]{2,1,0:T(8,128)(2,1)S(1)}, u32[]{:S(2)}, u32[]{:S(2)}) %all-to-all-start) | async-done | bytes 819232 | tf_op jit(solution)/shard_map/all_to_all | solution.py:28
  24.5 8.8 %collective-permute-done.1.refs_2_ = bf16[512,640]{1,0:T(8,128)(2,1)S(1)} collective-permute-done((bf16[512,640]{1,0:T(8,128)(2,1)}, bf16[512,640]{1,0:T(8,128)(2,1)S(1)}, u32[]{:S(2)}, u32[]{:S(2)}) %collective-permute-start.1) | collective-permute-done | bytes 655392 | tf_op jit(solution)/shard_map/ppermute | solution.py:33
  38.6 9.1 %collective-permute-done.4.refs_4_ = bf16[512,640]{1,0:T(8,128)(2,1)} collective-permute-done((bf16[512,640]{1,0:T(8,128)(2,1)S(1)}, bf16[512,640]{1,0:T(8,128)(2,1)}, u32[]{:S(2)}, u32[]{:S(2)}) %collective-permute-start.4) | collective-permute-done | bytes 655392 | tf_op jit(solution)/shard_map/ppermute | solution.py:44
  50.2 11.3 %hidden_and_sums.1 = (f32[1024,640]{1,0:T(8,128)}, f32[16,1024]{1,0:T(8,128)S(1)}, bf16[4096,640]{1,0:T(8,128)(2,1)}) custom-call(s32[3]{0:T(128)S(1)} %pad_add_fusion.where, bf16[512,640]{1,0:T(8,128)(2,1)} %refs_0_, bf16[512,640]{1,0:T(8,128)(2,1)} %collective-permute-done.refs_1_, bf16[512,640]{1,0:T(8,128)(2,1)} %copy-done.2, ...), custom_call_target="tpu_custom_call" | custom-call | flops 3355443200 | bytes 20971520 | tf_op jit(solution)/shard_map/hidden_and_sums/pallas_call | solution.py:186
  63.0 3.2 %collective-permute-start.13 = (f32[16,1024]{1,0:T(8,128)S(1)}, f32[16,1024]{1,0:T(8,128)S(1)}, u32[]{:S(2)}, u32[]{:S(2)}) collective-permute-start(f32[16,1024]{1,0:T(8,128)S(1)} %maximum_add_fusion), channel_id=1, source_target_pairs={{0,3},{1,0},{2,1},{3,2},{4,7},{5,4},{6,5},{7,6},{8,11},{9,8},{10,9... | collective-permute-start | bytes 196616 | tf_op jit(solution)/shard_map/ppermute | solution.py:33
  69.1 2.9 %collective-permute-done.14 = f32[16,1024]{1,0:T(8,128)S(1)} collective-permute-done((f32[16,1024]{1,0:T(8,128)S(1)}, f32[16,1024]{1,0:T(8,128)S(1)}, u32[]{:S(2)}, u32[]{:S(2)}) %collective-permute-start.14) | collective-permute-done | bytes 65568 | tf_op jit(solution)/shard_map/ppermute | solution.py:33
  75.4 2.5 %fusion.1 = f32[640,640]{1,0:T(8,128)S(1)} fusion(bf16[1024,640]{1,0:T(8,128)(2,1)S(1)} %subtract_convert_fusion, bf16[4096,640]{1,0:T(8,128)(2,1)} %get-tuple-element.44), kind=kOutput, calls=%fused_computation.3 | convolution fusion | flops 838860800 | bytes 4259840 | tf_op jit(solution)/shard_map/rd,rj->dj/dot_general | solution.py:275
  78.0 2.5 %fusion.3 = f32[640,640]{1,0:T(8,128)S(1)} fusion(bf16[1024,640]{1,0:T(8,128)(2,1)S(1)} %subtract_convert_fusion, bf16[4096,640]{1,0:T(8,128)(2,1)} %get-tuple-element.44), kind=kOutput, calls=%fused_computation.5 | convolution fusion | flops 838860800 | bytes 4259840 | tf_op jit(solution)/shard_map/rd,rj->dj/dot_general | solution.py:275
  82.6 2.5 %fusion.5 = f32[640,640]{1,0:T(8,128)S(1)} fusion(bf16[1024,640]{1,0:T(8,128)(2,1)S(1)} %subtract_convert_fusion, bf16[4096,640]{1,0:T(8,128)(2,1)} %get-tuple-element.44), kind=kOutput, calls=%fused_computation.7 | convolution fusion | flops 838860800 | bytes 4259840 | tf_op jit(solution)/shard_map/rd,rj->dj/dot_general | solution.py:275
  85.1 8.1 %collective-permute-done.25 = bf16[640,256]{1,0:T(8,128)(2,1)S(1)} collective-permute-done((bf16[640,256]{1,0:T(8,128)(2,1)S(1)}, bf16[640,256]{1,0:T(8,128)(2,1)S(1)}, u32[]{:S(2)}, u32[]{:S(2)}) %collective-permute-start.25) | collective-permute-done | bytes 327712 | tf_op jit(solution)/shard_map/ppermute | solution.py:45
  97.1 2.4 %collective-permute-start.16 = (bf16[680,384]{1,0:T(8,128)(2,1)S(1)}, bf16[680,384]{1,0:T(8,128)(2,1)S(1)}, u32[]{:S(2)}, u32[]{:S(2)}) collective-permute-start(bf16[680,384]{1,0:T(8,128)(2,1)S(1)} %fusion.26), channel_id=1, source_target_pairs={{0,64},{64,128},{128,192},{192,0},{1,65},{65,129},{129,193},{193,1... | collective-permute-start | bytes 1566728 | tf_op jit(solution)/shard_map/ppermute | solution.py:33
  99.5 4.6 %collective-permute-done.26 = bf16[640,256]{1,0:T(8,128)(2,1)S(1)} collective-permute-done((bf16[640,256]{1,0:T(8,128)(2,1)S(1)}, bf16[640,256]{1,0:T(8,128)(2,1)S(1)}, u32[]{:S(2)}, u32[]{:S(2)}) %collective-permute-start.26) | collective-permute-done | bytes 327712 | tf_op jit(solution)/shard_map/ppermute | solution.py:33
  104.1 2.9 %collective-permute-done.27 = bf16[640,256]{1,0:T(8,128)(2,1)S(1)} collective-permute-done((bf16[640,256]{1,0:T(8,128)(2,1)S(1)}, bf16[640,256]{1,0:T(8,128)(2,1)S(1)}, u32[]{:S(2)}, u32[]{:S(2)}) %collective-permute-start.27) | collective-permute-done | bytes 327712 | tf_op jit(solution)/shard_map/ppermute | solution.py:33
  107.2 6.9 %collective-permute-done.17 = bf16[680,384]{1,0:T(8,128)(2,1)S(1)} collective-permute-done((bf16[680,384]{1,0:T(8,128)(2,1)S(1)}, bf16[680,384]{1,0:T(8,128)(2,1)S(1)}, u32[]{:S(2)}, u32[]{:S(2)}) %collective-permute-start.17) | collective-permute-done | bytes 522272 | tf_op jit(solution)/shard_map/ppermute | solution.py:33
  114.7 7.3 %collective-permute-start.18 = (bf16[104,384]{1,0:T(8,128)(2,1)S(1)}, bf16[104,384]{1,0:T(8,128)(2,1)S(1)}, u32[]{:S(2)}, u32[]{:S(2)}) collective-permute-start(bf16[104,384]{1,0:T(8,128)(2,1)S(1)} %get-tuple-element.127), channel_id=1, source_target_pairs={{0,32},{8,40},{16,48},{24,56},{32,0},{40,8},{48,16},{56,24},{1,33}... | collective-permute-start | bytes 239624 | tf_op jit(solution)/shard_map/ppermute | solution.py:33
  121.9 1.9 %collective-permute-start.19 = (bf16[104,384]{1,0:T(8,128)(2,1)S(1)}, bf16[104,384]{1,0:T(8,128)(2,1)S(1)}, u32[]{:S(2)}, u32[]{:S(2)}) collective-permute-start(bf16[104,384]{1,0:T(8,128)(2,1)S(1)} %get-tuple-element.128), channel_id=1, source_target_pairs={{0,24},{8,32},{16,40},{24,48},{32,56},{40,0},{48,8},{56,16},{1,25}... | collective-permute-start | bytes 239624 | tf_op jit(solution)/shard_map/ppermute | solution.py:33
  123.9 3.1 %collective-permute-start.20 = (bf16[104,384]{1,0:T(8,128)(2,1)S(1)}, bf16[104,384]{1,0:T(8,128)(2,1)S(1)}, u32[]{:S(2)}, u32[]{:S(2)}) collective-permute-start(bf16[104,384]{1,0:T(8,128)(2,1)S(1)} %get-tuple-element.129), channel_id=1, source_target_pairs={{0,40},{8,48},{16,56},{24,0},{32,8},{40,16},{48,24},{56,32},{1,41}... | collective-permute-start | bytes 239624 | tf_op jit(solution)/shard_map/ppermute | solution.py:33
  128.4 2.7 %collective-permute-start.22 = (bf16[104,384]{1,0:T(8,128)(2,1)S(1)}, bf16[104,384]{1,0:T(8,128)(2,1)S(1)}, u32[]{:S(2)}, u32[]{:S(2)}) collective-permute-start(bf16[104,384]{1,0:T(8,128)(2,1)S(1)} %get-tuple-element.131), channel_id=1, source_target_pairs={{0,48},{8,56},{16,0},{24,8},{32,16},{40,24},{48,32},{56,40},{1,49}... | collective-permute-start | bytes 239624 | tf_op jit(solution)/shard_map/ppermute | solution.py:33
  135.2 3.4 %all-to-all-start.1 = ((bf16[8,80,256]{2,1,0:T(8,128)(2,1)}), bf16[8,80,256]{2,1,0:T(8,128)(2,1)S(1)}, u32[]{:S(2)}, u32[]{:S(2)}) async-start(bf16[8,80,256]{2,1,0:T(8,128)(2,1)} %broadcast_select_fusion.2), calls=%async_computation.1 | async-start | bytes 655360 | tf_op jit(solution)/shard_map/all_to_all | solution.py:28
  141.0 8.8 %all-to-all-done.1 = bf16[8,80,256]{2,1,0:T(8,128)(2,1)S(1)} async-done(((bf16[8,80,256]{2,1,0:T(8,128)(2,1)}), bf16[8,80,256]{2,1,0:T(8,128)(2,1)S(1)}, u32[]{:S(2)}, u32[]{:S(2)}) %all-to-all-start.1) | async-done | bytes 327712 | tf_op jit(solution)/shard_map/all_to_all | solution.py:28
  149.8 3.6 %collective-permute-start.28 = (bf16[80,640]{1,0:T(8,128)(2,1)S(1)}, bf16[80,640]{1,0:T(8,128)(2,1)S(1)}, u32[]{:S(2)}, u32[]{:S(2)}) collective-permute-start(bf16[80,640]{1,0:T(8,128)(2,1)S(1)} %pad_maximum_fusion.10), channel_id=1, source_target_pairs={{0,0},{1,65},{2,130},{3,195},{4,56},{5,121},{6,186},{7,251},{8,8},... | collective-permute-start | bytes 307208 | tf_op jit(solution)/shard_map/ppermute | solution.py:349
  154.6 5.5 %collective-permute-done.28 = bf16[80,640]{1,0:T(8,128)(2,1)S(1)} collective-permute-done((bf16[80,640]{1,0:T(8,128)(2,1)S(1)}, bf16[80,640]{1,0:T(8,128)(2,1)S(1)}, u32[]{:S(2)}, u32[]{:S(2)}) %collective-permute-start.28) | collective-permute-done | bytes 102432 | tf_op jit(solution)/shard_map/ppermute | solution.py:349
  (153 shorter events, 37.5 us)
Async XLA Ops:
  3.6 18.7 %all-to-all-start = ((bf16[4,160,640]{2,1,0:T(8,128)(2,1)}), bf16[4,160,640]{2,1,0:T(8,128)(2,1)S(1)}, u32[]{:S(2)}, u32[]{:S(2)}) async-start(bf16[4,160,640]{2,1,0:T(8,128)(2,1)} %pad_maximum_fusion), calls=%async_computation | async-start | bytes 1638400 | tf_op jit(solution)/shard_map/all_to_all | solution.py:28
  8.2 25.2 %collective-permute-start.1 = (bf16[512,640]{1,0:T(8,128)(2,1)}, bf16[512,640]{1,0:T(8,128)(2,1)S(1)}, u32[]{:S(2)}, u32[]{:S(2)}) collective-permute-start(bf16[512,640]{1,0:T(8,128)(2,1)} %refs_0_), channel_id=1, source_target_pairs={{0,3},{1,0},{2,1},{3,2},{4,7},{5,4},{6,5},{7,6},{8,11},{9,8},{10,9... | collective-permute-start | bytes 1966088 | tf_op jit(solution)/shard_map/ppermute | solution.py:33
  11.4 23.2 %collective-permute-start.3 = (bf16[512,640]{1,0:T(8,128)(2,1)}, bf16[512,640]{1,0:T(8,128)(2,1)}, u32[]{:S(2)}, u32[]{:S(2)}) collective-permute-start(bf16[512,640]{1,0:T(8,128)(2,1)} %refs_0_), channel_id=1, source_target_pairs={{0,1},{1,2},{2,3},{3,0},{4,5},{5,6},{6,7},{7,4},{8,9},{9,10},{10,1... | collective-permute-start | bytes 1966088 | tf_op jit(solution)/shard_map/ppermute | solution.py:33
  12.4 25.7 %collective-permute-start.10 = (bf16[520,640]{1,0:T(8,128)(2,1)}, bf16[520,640]{1,0:T(8,128)(2,1)}, u32[]{:S(2)}, u32[]{:S(2)}) collective-permute-start(bf16[520,640]{1,0:T(8,128)(2,1)} %fusion.17), channel_id=1, source_target_pairs={{0,4},{4,0},{1,5},{5,1},{2,6},{6,2},{3,7},{7,3},{8,12},{12,8},{9,1... | collective-permute-start | bytes 1996808 | tf_op jit(solution)/shard_map/ppermute | solution.py:37
  22.4 14.1 %collective-permute-start.7 = (bf16[3,160,640]{2,1,0:T(8,128)(2,1)S(1)}, bf16[3,160,640]{2,1,0:T(8,128)(2,1)S(1)}, u32[]{:S(2)}, u32[]{:S(2)}) collective-permute-start(bf16[3,160,640]{2,1,0:T(8,128)(2,1)S(1)} %pad_maximum_fusion.1.refs_9_), channel_id=1, source_target_pairs={{0,64},{64,128},{128,192},{192,0},{1,65},{65,129},{129,193},{193,1... | collective-permute-start | bytes 1843208 | tf_op jit(solution)/shard_map/ppermute | solution.py:33
  23.7 13.4 %collective-permute-start.8 = (bf16[3,160,640]{2,1,0:T(8,128)(2,1)S(1)}, bf16[3,160,640]{2,1,0:T(8,128)(2,1)S(1)}, u32[]{:S(2)}, u32[]{:S(2)}) collective-permute-start(bf16[3,160,640]{2,1,0:T(8,128)(2,1)S(1)} %pad_maximum_fusion.1.refs_9_), channel_id=1, source_target_pairs={{0,192},{64,0},{128,64},{192,128},{1,193},{65,1},{129,65},{193,129... | collective-permute-start | bytes 1843208 | tf_op jit(solution)/shard_map/ppermute | solution.py:33
  35.8 12.0 %collective-permute-start.4 = (bf16[512,640]{1,0:T(8,128)(2,1)S(1)}, bf16[512,640]{1,0:T(8,128)(2,1)}, u32[]{:S(2)}, u32[]{:S(2)}) collective-permute-start(bf16[512,640]{1,0:T(8,128)(2,1)S(1)} %broadcast_select_fusion), channel_id=1, source_target_pairs={{0,1},{1,2},{2,3},{3,0},{4,7},{5,4},{6,5},{7,6},{8,9},{9,10},{10,1... | collective-permute-start | bytes 1966088 | tf_op jit(solution)/shard_map/ppermute | solution.py:44
  36.3 12.8 %collective-permute-start = (bf16[512,640]{1,0:T(8,128)(2,1)}, bf16[512,640]{1,0:T(8,128)(2,1)}, u32[]{:S(2)}, u32[]{:S(2)}) collective-permute-start(bf16[512,640]{1,0:T(8,128)(2,1)} %refs_0_), channel_id=1, source_target_pairs={{0,4},{4,0},{1,5},{5,1},{2,6},{6,2},{3,7},{7,3},{8,12},{12,8},{9,1... | collective-permute-start | bytes 1966088 | tf_op jit(solution)/shard_map/ppermute | solution.py:37
  36.5 12.5 %collective-permute-start.2 = (bf16[512,640]{1,0:T(8,128)(2,1)S(1)}, bf16[512,640]{1,0:T(8,128)(2,1)}, u32[]{:S(2)}, u32[]{:S(2)}) collective-permute-start(bf16[512,640]{1,0:T(8,128)(2,1)S(1)} %collective-permute-done.1.refs_2_), channel_id=1, source_target_pairs={{0,4},{4,0},{1,5},{5,1},{2,6},{6,2},{3,7},{7,3},{8,12},{12,8},{9,1... | collective-permute-start | bytes 1966088 | tf_op jit(solution)/shard_map/ppermute | solution.py:37
  37.1 11.9 %collective-permute-start.6 = (bf16[512,640]{1,0:T(8,128)(2,1)}, bf16[512,640]{1,0:T(8,128)(2,1)}, u32[]{:S(2)}, u32[]{:S(2)}) collective-permute-start(bf16[512,640]{1,0:T(8,128)(2,1)} %collective-permute-done.3.refs_6_), channel_id=1, source_target_pairs={{0,4},{4,0},{1,5},{5,1},{2,6},{6,2},{3,7},{7,3},{8,12},{12,8},{9,1... | collective-permute-start | bytes 1966088 | tf_op jit(solution)/shard_map/ppermute | solution.py:37
  38.1 10.9 %collective-permute-start.9 = (bf16[3,160,640]{2,1,0:T(8,128)(2,1)}, bf16[3,160,640]{2,1,0:T(8,128)(2,1)}, u32[]{:S(2)}, u32[]{:S(2)}) collective-permute-start(bf16[3,160,640]{2,1,0:T(8,128)(2,1)} %broadcast_select_fusion.1), channel_id=1, source_target_pairs={{0,64},{64,128},{128,192},{192,0},{4,196},{68,4},{132,68},{196,132... | collective-permute-start | bytes 1843208 | tf_op jit(solution)/shard_map/ppermute | solution.py:45
  80.5 15.0 %collective-permute-start.15 = (bf16[680,384]{1,0:T(8,128)(2,1)S(1)}, bf16[680,384]{1,0:T(8,128)(2,1)S(1)}, u32[]{:S(2)}, u32[]{:S(2)}) collective-permute-start(bf16[680,384]{1,0:T(8,128)(2,1)S(1)} %fusion.25), channel_id=1, source_target_pairs={{0,64},{64,128},{128,192},{192,0},{4,196},{68,4},{132,68},{196,132... | collective-permute-start | bytes 1566728 | tf_op jit(solution)/shard_map/ppermute | solution.py:45
  81.1 12.2 %collective-permute-start.25 = (bf16[640,256]{1,0:T(8,128)(2,1)S(1)}, bf16[640,256]{1,0:T(8,128)(2,1)S(1)}, u32[]{:S(2)}, u32[]{:S(2)}) collective-permute-start(bf16[640,256]{1,0:T(8,128)(2,1)S(1)} %convolution_convert_fusion.1), channel_id=1, source_target_pairs={{0,64},{64,128},{128,192},{192,0},{4,196},{68,4},{132,68},{196,132... | collective-permute-start | bytes 983048 | tf_op jit(solution)/shard_map/ppermute | solution.py:45
  93.4 10.7 %collective-permute-start.26 = (bf16[640,256]{1,0:T(8,128)(2,1)S(1)}, bf16[640,256]{1,0:T(8,128)(2,1)S(1)}, u32[]{:S(2)}, u32[]{:S(2)}) collective-permute-start(bf16[640,256]{1,0:T(8,128)(2,1)S(1)} %get-tuple-element.56), channel_id=1, source_target_pairs={{0,64},{64,128},{128,192},{192,0},{1,65},{65,129},{129,193},{193,1... | collective-permute-start | bytes 983048 | tf_op jit(solution)/shard_map/ppermute | solution.py:33
  95.2 11.8 %collective-permute-start.27 = (bf16[640,256]{1,0:T(8,128)(2,1)S(1)}, bf16[640,256]{1,0:T(8,128)(2,1)S(1)}, u32[]{:S(2)}, u32[]{:S(2)}) collective-permute-start(bf16[640,256]{1,0:T(8,128)(2,1)S(1)} %get-tuple-element.57), channel_id=1, source_target_pairs={{0,192},{64,0},{128,64},{192,128},{1,193},{65,1},{129,65},{193,129... | collective-permute-start | bytes 983048 | tf_op jit(solution)/shard_map/ppermute | solution.py:33
  96.2 17.9 %collective-permute-start.17 = (bf16[680,384]{1,0:T(8,128)(2,1)S(1)}, bf16[680,384]{1,0:T(8,128)(2,1)S(1)}, u32[]{:S(2)}, u32[]{:S(2)}) collective-permute-start(bf16[680,384]{1,0:T(8,128)(2,1)S(1)} %fusion.27), channel_id=1, source_target_pairs={{0,192},{64,0},{128,64},{192,128},{1,193},{65,1},{129,65},{193,129... | collective-permute-start | bytes 1566728 | tf_op jit(solution)/shard_map/ppermute | solution.py:33
  97.1 17.0 %collective-permute-start.16 = (bf16[680,384]{1,0:T(8,128)(2,1)S(1)}, bf16[680,384]{1,0:T(8,128)(2,1)S(1)}, u32[]{:S(2)}, u32[]{:S(2)}) collective-permute-start(bf16[680,384]{1,0:T(8,128)(2,1)S(1)} %fusion.26), channel_id=1, source_target_pairs={{0,64},{64,128},{128,192},{192,0},{1,65},{65,129},{129,193},{193,1... | collective-permute-start | bytes 1566728 | tf_op jit(solution)/shard_map/ppermute | solution.py:33
  114.7 16.5 %collective-permute-start.18 = (bf16[104,384]{1,0:T(8,128)(2,1)S(1)}, bf16[104,384]{1,0:T(8,128)(2,1)S(1)}, u32[]{:S(2)}, u32[]{:S(2)}) collective-permute-start(bf16[104,384]{1,0:T(8,128)(2,1)S(1)} %get-tuple-element.127), channel_id=1, source_target_pairs={{0,32},{8,40},{16,48},{24,56},{32,0},{40,8},{48,16},{56,24},{1,33}... | collective-permute-start | bytes 239624 | tf_op jit(solution)/shard_map/ppermute | solution.py:33
  121.9 10.6 %collective-permute-start.19 = (bf16[104,384]{1,0:T(8,128)(2,1)S(1)}, bf16[104,384]{1,0:T(8,128)(2,1)S(1)}, u32[]{:S(2)}, u32[]{:S(2)}) collective-permute-start(bf16[104,384]{1,0:T(8,128)(2,1)S(1)} %get-tuple-element.128), channel_id=1, source_target_pairs={{0,24},{8,32},{16,40},{24,48},{32,56},{40,0},{48,8},{56,16},{1,25}... | collective-permute-start | bytes 239624 | tf_op jit(solution)/shard_map/ppermute | solution.py:33
  123.9 14.8 %collective-permute-start.20 = (bf16[104,384]{1,0:T(8,128)(2,1)S(1)}, bf16[104,384]{1,0:T(8,128)(2,1)S(1)}, u32[]{:S(2)}, u32[]{:S(2)}) collective-permute-start(bf16[104,384]{1,0:T(8,128)(2,1)S(1)} %get-tuple-element.129), channel_id=1, source_target_pairs={{0,40},{8,48},{16,56},{24,0},{32,8},{40,16},{48,24},{56,32},{1,41}... | collective-permute-start | bytes 239624 | tf_op jit(solution)/shard_map/ppermute | solution.py:33
  127.0 11.7 %collective-permute-start.21 = (bf16[104,384]{1,0:T(8,128)(2,1)S(1)}, bf16[104,384]{1,0:T(8,128)(2,1)S(1)}, u32[]{:S(2)}, u32[]{:S(2)}) collective-permute-start(bf16[104,384]{1,0:T(8,128)(2,1)S(1)} %get-tuple-element.130), channel_id=1, source_target_pairs={{0,16},{8,24},{16,32},{24,40},{32,48},{40,56},{48,0},{56,8},{1,17}... | collective-permute-start | bytes 239624 | tf_op jit(solution)/shard_map/ppermute | solution.py:33
  128.4 10.2 %collective-permute-start.22 = (bf16[104,384]{1,0:T(8,128)(2,1)S(1)}, bf16[104,384]{1,0:T(8,128)(2,1)S(1)}, u32[]{:S(2)}, u32[]{:S(2)}) collective-permute-start(bf16[104,384]{1,0:T(8,128)(2,1)S(1)} %get-tuple-element.131), channel_id=1, source_target_pairs={{0,48},{8,56},{16,0},{24,8},{32,16},{40,24},{48,32},{56,40},{1,49}... | collective-permute-start | bytes 239624 | tf_op jit(solution)/shard_map/ppermute | solution.py:33
  135.2 14.5 %all-to-all-start.1 = ((bf16[8,80,256]{2,1,0:T(8,128)(2,1)}), bf16[8,80,256]{2,1,0:T(8,128)(2,1)S(1)}, u32[]{:S(2)}, u32[]{:S(2)}) async-start(bf16[8,80,256]{2,1,0:T(8,128)(2,1)} %broadcast_select_fusion.2), calls=%async_computation.1 | async-start | bytes 655360 | tf_op jit(solution)/shard_map/all_to_all | solution.py:28
  149.8 10.3 %collective-permute-start.28 = (bf16[80,640]{1,0:T(8,128)(2,1)S(1)}, bf16[80,640]{1,0:T(8,128)(2,1)S(1)}, u32[]{:S(2)}, u32[]{:S(2)}) collective-permute-start(bf16[80,640]{1,0:T(8,128)(2,1)S(1)} %pad_maximum_fusion.10), channel_id=1, source_target_pairs={{0,0},{1,65},{2,130},{3,195},{4,56},{5,121},{6,186},{7,251},{8,8},... | collective-permute-start | bytes 307208 | tf_op jit(solution)/shard_map/ppermute | solution.py:349
  (15 other events, 103.6 us)

commit v2 on v1

--- a/solution.py
+++ b/solution.py
@@ -121,8 +121,8 @@
 
 def hidden_kernel(where, *refs):
     rows, refs = refs[: NC * NY], refs[NC * NY :]
-    out_proj, w_own, w_low, w_high, w_far, resid, pack, gh, hidden, sums, *refs = refs
-    turned, a, w, res, sem = refs
+    out_proj, w_own, w_low, w_high, w_far, resid, pack, gh, hidden_out, sums, *refs = refs
+    turned, a, w, res, hidden, sem = refs
     y, c, x = where[0], where[1], where[2]
     count, half = rows[0].shape
     part = w_own.shape[1]
@@ -161,19 +161,29 @@
             tile = jnp.where(lane == members, squares, tile).T
             sums[:, here] = tile[: 2 * members]
 
+    whole = NC * count
+
+    def turn(rows):
+        return [
+            fetch(
+                a.at[rows, columns(lax.rem(x + s, NX))],
+                turned.at[s * whole + rows.start : s * whole + rows.stop],
+            )
+            for s in range(NX)
+        ]
+
     for copy in ready[:early]:
         copy.wait()
+    out = turn(halves[0])
     multiply(0)
     for copy in ready[early:]:
         copy.wait()
-    whole = NC * count
-    moved = [
-        fetch(a.at[:, columns(lax.rem(x + s, NX))], turned.at[s * whole : (s + 1) * whole])
-        for s in range(NX)
-    ]
+    out += turn(halves[1])
+    out.append(fetch(hidden.at[halves[0]], hidden_out.at[halves[0]]))
     multiply(count)
-    for copy in moved:
+    for copy in out:
         copy.wait()
+    fetch(hidden.at[halves[1]], hidden_out.at[halves[1]]).wait()
 
 
 def hidden_and_sums(where, rows, out_proj, weights, resid, pack, gh):
@@ -189,12 +199,13 @@
             num_scalar_prefetch=1,
             grid=(1,),
             in_specs=[any_space] * (NC * NY + 7) + [full(gh.shape)],
-            out_specs=[full((total, half)), full((2 * members, total)), any_space],
+            out_specs=[any_space, full((2 * members, total)), any_space],
             scratch_shapes=[
                 pltpu.VMEM((total, NY * half), BF),
                 pltpu.VMEM((NY, half, half), BF),
                 pltpu.VMEM((total, half), BF),
-                pltpu.SemaphoreType.DMA((24,)),
+                pltpu.VMEM((total, half), F32),
+                pltpu.SemaphoreType.DMA((25,)),
             ],
         ),
         out_shape=[

time: 161 us -> 161 us (level)
  no operation moved by 1% of the time
where the time goes in v2:
time: 161 us; the launch traced here: 160 us
  waiting for transfers between devices  73.4 us (46%)
  starting transfers between devices  49 us (30%)
  Pallas kernels  10.9 us (7%)
  other arithmetic  10.6 us (7%)
  matrix products  10.5 us (7%)
  local copies, waits for them, and re-layouts  4.41 us (3%)
    ppermute x18, starting transfers between devices, shift(): return lax.ppermute(x, axis, [(i, (i + by) % n) for i in range(n)])  33.5 us
    ppermute x18, waiting for transfers between devices, shift(): return lax.ppermute(x, axis, [(i, (i + by) % n) for i in range(n)])  29.6 us
    all_to_all x2, waiting for transfers between devices, exchanged(): return lax.all_to_all(x, axis, split_axis=0, concat_axis=0, tiled=True)  18.6 us
    pallas_call x1, Pallas kernels, hidden_and_sums(): pl.pallas_call(hidden_kernel, grid_spec=pltpu.PrefetchScalarGridSpec(num_...  10.9 us
    ppermute x1, waiting for transfers between devices, shift_by_core(): lax.ppermute(x, ('c', axis), [(c * n + i, c * n + j) for c, i, j in moves])  9.15 us
    dot_general x5, matrix products, term(): return jnp.einsum('rd,rj->dj', left, right, preferred_element_type=F32)  9.07 us
    ppermute x3, waiting for transfers between devices, shift_by_core(): lax.ppermute(x, (axis, 'c'), [(i * NC + c, j * NC + c) for c, i, j in mov...  8.14 us
    all_to_all x2, starting transfers between devices, exchanged(): return lax.all_to_all(x, axis, split_axis=0, concat_axis=0, tiled=True)  8.03 us
  transfers between devices with their start and end apart: 32, of which 18 were waited for; matrix products, arithmetic and copies ran while one was open for 8% of the time, Pallas kernels for 0%

profile of v2, /device:TPU:6, one launch (start us, length us, event | category | flops | bytes accessed | tf_op | source)
XLA Modules:
  0.0 160.4 jit_solution(9757358909939689777)
XLA Ops:
  3.6 4.6 %all-to-all-start = ((bf16[4,160,640]{2,1,0:T(8,128)(2,1)}), bf16[4,160,640]{2,1,0:T(8,128)(2,1)S(1)}, u32[]{:S(2)}, u32[]{:S(2)}) async-start(bf16[4,160,640]{2,1,0:T(8,128)(2,1)} %pad_maximum_fusion), calls=%async_computation | async-start | bytes 1638400 | tf_op jit(solution)/shard_map/all_to_all | solution.py:28
  8.2 3.2 %collective-permute-start.1 = (bf16[512,640]{1,0:T(8,128)(2,1)}, bf16[512,640]{1,0:T(8,128)(2,1)S(1)}, u32[]{:S(2)}, u32[]{:S(2)}) collective-permute-start(bf16[512,640]{1,0:T(8,128)(2,1)} %refs_0_), channel_id=1, source_target_pairs={{0,3},{1,0},{2,1},{3,2},{4,7},{5,4},{6,5},{7,6},{8,11},{9,8},{10,9... | collective-permute-start | bytes 1966088 | tf_op jit(solution)/shard_map/ppermute | solution.py:33
  12.4 9.9 %all-to-all-done = bf16[4,160,640]{2,1,0:T(8,128)(2,1)S(1)} async-done(((bf16[4,160,640]{2,1,0:T(8,128)(2,1)}), bf16[4,160,640]{2,1,0:T(8,128)(2,1)S(1)}, u32[]{:S(2)}, u32[]{:S(2)}) %all-to-all-start) | async-done | bytes 819232 | tf_op jit(solution)/shard_map/all_to_all | solution.py:28
  24.5 8.8 %collective-permute-done.1.refs_2_ = bf16[512,640]{1,0:T(8,128)(2,1)S(1)} collective-permute-done((bf16[512,640]{1,0:T(8,128)(2,1)}, bf16[512,640]{1,0:T(8,128)(2,1)S(1)}, u32[]{:S(2)}, u32[]{:S(2)}) %collective-permute-start.1) | collective-permute-done | bytes 655392 | tf_op jit(solution)/shard_map/ppermute | solution.py:33
  38.6 9.1 %collective-permute-done.4.refs_4_ = bf16[512,640]{1,0:T(8,128)(2,1)} collective-permute-done((bf16[512,640]{1,0:T(8,128)(2,1)S(1)}, bf16[512,640]{1,0:T(8,128)(2,1)}, u32[]{:S(2)}, u32[]{:S(2)}) %collective-permute-start.4) | collective-permute-done | bytes 655392 | tf_op jit(solution)/shard_map/ppermute | solution.py:44
  50.2 10.9 %hidden_and_sums.1 = (f32[1024,640]{1,0:T(8,128)}, f32[16,1024]{1,0:T(8,128)S(1)}, bf16[4096,640]{1,0:T(8,128)(2,1)}) custom-call(s32[3]{0:T(128)S(1)} %pad_add_fusion.where, bf16[512,640]{1,0:T(8,128)(2,1)} %refs_0_, bf16[512,640]{1,0:T(8,128)(2,1)} %collective-permute-done.refs_1_, bf16[512,640]{1,0:T(8,128)(2,1)} %copy-done.2, ...), custom_call_target="tpu_custom_call" | custom-call | flops 3355443200 | bytes 20971520 | tf_op jit(solution)/shard_map/hidden_and_sums/pallas_call | solution.py:196
  62.6 3.2 %collective-permute-start.13 = (f32[16,1024]{1,0:T(8,128)S(1)}, f32[16,1024]{1,0:T(8,128)S(1)}, u32[]{:S(2)}, u32[]{:S(2)}) collective-permute-start(f32[16,1024]{1,0:T(8,128)S(1)} %maximum_add_fusion), channel_id=1, source_target_pairs={{0,3},{1,0},{2,1},{3,2},{4,7},{5,4},{6,5},{7,6},{8,11},{9,8},{10,9... | collective-permute-start | bytes 196616 | tf_op jit(solution)/shard_map/ppermute | solution.py:33
  68.7 2.9 %collective-permute-done.14 = f32[16,1024]{1,0:T(8,128)S(1)} collective-permute-done((f32[16,1024]{1,0:T(8,128)S(1)}, f32[16,1024]{1,0:T(8,128)S(1)}, u32[]{:S(2)}, u32[]{:S(2)}) %collective-permute-start.14) | collective-permute-done | bytes 65568 | tf_op jit(solution)/shard_map/ppermute | solution.py:33
  75.0 2.5 %fusion.1 = f32[640,640]{1,0:T(8,128)S(1)} fusion(bf16[1024,640]{1,0:T(8,128)(2,1)S(1)} %subtract_convert_fusion, bf16[4096,640]{1,0:T(8,128)(2,1)} %get-tuple-element.44), kind=kOutput, calls=%fused_computation.3 | convolution fusion | flops 838860800 | bytes 4259840 | tf_op jit(solution)/shard_map/rd,rj->dj/dot_general | solution.py:286
  77.6 2.5 %fusion.3 = f32[640,640]{1,0:T(8,128)S(1)} fusion(bf16[1024,640]{1,0:T(8,128)(2,1)S(1)} %subtract_convert_fusion, bf16[4096,640]{1,0:T(8,128)(2,1)} %get-tuple-element.44), kind=kOutput, calls=%fused_computation.5 | convolution fusion | flops 838860800 | bytes 4259840 | tf_op jit(solution)/shard_map/rd,rj->dj/dot_general | solution.py:286
  82.2 2.5 %fusion.5 = f32[640,640]{1,0:T(8,128)S(1)} fusion(bf16[1024,640]{1,0:T(8,128)(2,1)S(1)} %subtract_convert_fusion, bf16[4096,640]{1,0:T(8,128)(2,1)} %get-tuple-element.44), kind=kOutput, calls=%fused_computation.7 | convolution fusion | flops 838860800 | bytes 4259840 | tf_op jit(solution)/shard_map/rd,rj->dj/dot_general | solution.py:286
  84.7 8.1 %collective-permute-done.25 = bf16[640,256]{1,0:T(8,128)(2,1)S(1)} collective-permute-done((bf16[640,256]{1,0:T(8,128)(2,1)S(1)}, bf16[640,256]{1,0:T(8,128)(2,1)S(1)}, u32[]{:S(2)}, u32[]{:S(2)}) %collective-permute-start.25) | collective-permute-done | bytes 327712 | tf_op jit(solution)/shard_map/ppermute | solution.py:45
  96.7 2.4 %collective-permute-start.16 = (bf16[680,384]{1,0:T(8,128)(2,1)S(1)}, bf16[680,384]{1,0:T(8,128)(2,1)S(1)}, u32[]{:S(2)}, u32[]{:S(2)}) collective-permute-start(bf16[680,384]{1,0:T(8,128)(2,1)S(1)} %fusion.26), channel_id=1, source_target_pairs={{0,64},{64,128},{128,192},{192,0},{1,65},{65,129},{129,193},{193,1... | collective-permute-start | bytes 1566728 | tf_op jit(solution)/shard_map/ppermute | solution.py:33
  99.1 4.5 %collective-permute-done.26 = bf16[640,256]{1,0:T(8,128)(2,1)S(1)} collective-permute-done((bf16[640,256]{1,0:T(8,128)(2,1)S(1)}, bf16[640,256]{1,0:T(8,128)(2,1)S(1)}, u32[]{:S(2)}, u32[]{:S(2)}) %collective-permute-start.26) | collective-permute-done | bytes 327712 | tf_op jit(solution)/shard_map/ppermute | solution.py:33
  103.7 2.9 %collective-permute-done.27 = bf16[640,256]{1,0:T(8,128)(2,1)S(1)} collective-permute-done((bf16[640,256]{1,0:T(8,128)(2,1)S(1)}, bf16[640,256]{1,0:T(8,128)(2,1)S(1)}, u32[]{:S(2)}, u32[]{:S(2)}) %collective-permute-start.27) | collective-permute-done | bytes 327712 | tf_op jit(solution)/shard_map/ppermute | solution.py:33
  106.9 6.9 %collective-permute-done.17 = bf16[680,384]{1,0:T(8,128)(2,1)S(1)} collective-permute-done((bf16[680,384]{1,0:T(8,128)(2,1)S(1)}, bf16[680,384]{1,0:T(8,128)(2,1)S(1)}, u32[]{:S(2)}, u32[]{:S(2)}) %collective-permute-start.17) | collective-permute-done | bytes 522272 | tf_op jit(solution)/shard_map/ppermute | solution.py:33
  114.3 7.3 %collective-permute-start.18 = (bf16[104,384]{1,0:T(8,128)(2,1)S(1)}, bf16[104,384]{1,0:T(8,128)(2,1)S(1)}, u32[]{:S(2)}, u32[]{:S(2)}) collective-permute-start(bf16[104,384]{1,0:T(8,128)(2,1)S(1)} %get-tuple-element.127), channel_id=1, source_target_pairs={{0,32},{8,40},{16,48},{24,56},{32,0},{40,8},{48,16},{56,24},{1,33}... | collective-permute-start | bytes 239624 | tf_op jit(solution)/shard_map/ppermute | solution.py:33
  121.6 1.9 %collective-permute-start.19 = (bf16[104,384]{1,0:T(8,128)(2,1)S(1)}, bf16[104,384]{1,0:T(8,128)(2,1)S(1)}, u32[]{:S(2)}, u32[]{:S(2)}) collective-permute-start(bf16[104,384]{1,0:T(8,128)(2,1)S(1)} %get-tuple-element.128), channel_id=1, source_target_pairs={{0,24},{8,32},{16,40},{24,48},{32,56},{40,0},{48,8},{56,16},{1,25}... | collective-permute-start | bytes 239624 | tf_op jit(solution)/shard_map/ppermute | solution.py:33
  123.5 3.1 %collective-permute-start.20 = (bf16[104,384]{1,0:T(8,128)(2,1)S(1)}, bf16[104,384]{1,0:T(8,128)(2,1)S(1)}, u32[]{:S(2)}, u32[]{:S(2)}) collective-permute-start(bf16[104,384]{1,0:T(8,128)(2,1)S(1)} %get-tuple-element.129), channel_id=1, source_target_pairs={{0,40},{8,48},{16,56},{24,0},{32,8},{40,16},{48,24},{56,32},{1,41}... | collective-permute-start | bytes 239624 | tf_op jit(solution)/shard_map/ppermute | solution.py:33
  128.1 2.7 %collective-permute-start.22 = (bf16[104,384]{1,0:T(8,128)(2,1)S(1)}, bf16[104,384]{1,0:T(8,128)(2,1)S(1)}, u32[]{:S(2)}, u32[]{:S(2)}) collective-permute-start(bf16[104,384]{1,0:T(8,128)(2,1)S(1)} %get-tuple-element.131), channel_id=1, source_target_pairs={{0,48},{8,56},{16,0},{24,8},{32,16},{40,24},{48,32},{56,40},{1,49}... | collective-permute-start | bytes 239624 | tf_op jit(solution)/shard_map/ppermute | solution.py:33
  134.8 3.4 %all-to-all-start.1 = ((bf16[8,80,256]{2,1,0:T(8,128)(2,1)}), bf16[8,80,256]{2,1,0:T(8,128)(2,1)S(1)}, u32[]{:S(2)}, u32[]{:S(2)}) async-start(bf16[8,80,256]{2,1,0:T(8,128)(2,1)} %broadcast_select_fusion.2), calls=%async_computation.1 | async-start | bytes 655360 | tf_op jit(solution)/shard_map/all_to_all | solution.py:28
  140.6 8.7 %all-to-all-done.1 = bf16[8,80,256]{2,1,0:T(8,128)(2,1)S(1)} async-done(((bf16[8,80,256]{2,1,0:T(8,128)(2,1)}), bf16[8,80,256]{2,1,0:T(8,128)(2,1)S(1)}, u32[]{:S(2)}, u32[]{:S(2)}) %all-to-all-start.1) | async-done | bytes 327712 | tf_op jit(solution)/shard_map/all_to_all | solution.py:28
  149.4 3.5 %collective-permute-start.28 = (bf16[80,640]{1,0:T(8,128)(2,1)S(1)}, bf16[80,640]{1,0:T(8,128)(2,1)S(1)}, u32[]{:S(2)}, u32[]{:S(2)}) collective-permute-start(bf16[80,640]{1,0:T(8,128)(2,1)S(1)} %pad_maximum_fusion.10), channel_id=1, source_target_pairs={{0,0},{1,65},{2,130},{3,195},{4,56},{5,121},{6,186},{7,251},{8,8},... | collective-permute-start | bytes 307208 | tf_op jit(solution)/shard_map/ppermute | solution.py:360
  154.2 5.5 %collective-permute-done.28 = bf16[80,640]{1,0:T(8,128)(2,1)S(1)} collective-permute-done((bf16[80,640]{1,0:T(8,128)(2,1)S(1)}, bf16[80,640]{1,0:T(8,128)(2,1)S(1)}, u32[]{:S(2)}, u32[]{:S(2)}) %collective-permute-start.28) | collective-permute-done | bytes 102432 | tf_op jit(solution)/shard_map/ppermute | solution.py:360
  (153 shorter events, 37.5 us)
Async XLA Ops:
  3.6 18.7 %all-to-all-start = ((bf16[4,160,640]{2,1,0:T(8,128)(2,1)}), bf16[4,160,640]{2,1,0:T(8,128)(2,1)S(1)}, u32[]{:S(2)}, u32[]{:S(2)}) async-start(bf16[4,160,640]{2,1,0:T(8,128)(2,1)} %pad_maximum_fusion), calls=%async_computation | async-start | bytes 1638400 | tf_op jit(solution)/shard_map/all_to_all | solution.py:28
  8.2 25.2 %collective-permute-start.1 = (bf16[512,640]{1,0:T(8,128)(2,1)}, bf16[512,640]{1,0:T(8,128)(2,1)S(1)}, u32[]{:S(2)}, u32[]{:S(2)}) collective-permute-start(bf16[512,640]{1,0:T(8,128)(2,1)} %refs_0_), channel_id=1, source_target_pairs={{0,3},{1,0},{2,1},{3,2},{4,7},{5,4},{6,5},{7,6},{8,11},{9,8},{10,9... | collective-permute-start | bytes 1966088 | tf_op jit(solution)/shard_map/ppermute | solution.py:33
  11.4 23.2 %collective-permute-start.3 = (bf16[512,640]{1,0:T(8,128)(2,1)}, bf16[512,640]{1,0:T(8,128)(2,1)}, u32[]{:S(2)}, u32[]{:S(2)}) collective-permute-start(bf16[512,640]{1,0:T(8,128)(2,1)} %refs_0_), channel_id=1, source_target_pairs={{0,1},{1,2},{2,3},{3,0},{4,5},{5,6},{6,7},{7,4},{8,9},{9,10},{10,1... | collective-permute-start | bytes 1966088 | tf_op jit(solution)/shard_map/ppermute | solution.py:33
  12.4 25.7 %collective-permute-start.10 = (bf16[520,640]{1,0:T(8,128)(2,1)}, bf16[520,640]{1,0:T(8,128)(2,1)}, u32[]{:S(2)}, u32[]{:S(2)}) collective-permute-start(bf16[520,640]{1,0:T(8,128)(2,1)} %fusion.17), channel_id=1, source_target_pairs={{0,4},{4,0},{1,5},{5,1},{2,6},{6,2},{3,7},{7,3},{8,12},{12,8},{9,1... | collective-permute-start | bytes 1996808 | tf_op jit(solution)/shard_map/ppermute | solution.py:37
  22.4 14.1 %collective-permute-start.7 = (bf16[3,160,640]{2,1,0:T(8,128)(2,1)S(1)}, bf16[3,160,640]{2,1,0:T(8,128)(2,1)S(1)}, u32[]{:S(2)}, u32[]{:S(2)}) collective-permute-start(bf16[3,160,640]{2,1,0:T(8,128)(2,1)S(1)} %pad_maximum_fusion.1.refs_9_), channel_id=1, source_target_pairs={{0,64},{64,128},{128,192},{192,0},{1,65},{65,129},{129,193},{193,1... | collective-permute-start | bytes 1843208 | tf_op jit(solution)/shard_map/ppermute | solution.py:33
  23.7 13.4 %collective-permute-start.8 = (bf16[3,160,640]{2,1,0:T(8,128)(2,1)S(1)}, bf16[3,160,640]{2,1,0:T(8,128)(2,1)S(1)}, u32[]{:S(2)}, u32[]{:S(2)}) collective-permute-start(bf16[3,160,640]{2,1,0:T(8,128)(2,1)S(1)} %pad_maximum_fusion.1.refs_9_), channel_id=1, source_target_pairs={{0,192},{64,0},{128,64},{192,128},{1,193},{65,1},{129,65},{193,129... | collective-permute-start | bytes 1843208 | tf_op jit(solution)/shard_map/ppermute | solution.py:33
  35.8 12.0 %collective-permute-start.4 = (bf16[512,640]{1,0:T(8,128)(2,1)S(1)}, bf16[512,640]{1,0:T(8,128)(2,1)}, u32[]{:S(2)}, u32[]{:S(2)}) collective-permute-start(bf16[512,640]{1,0:T(8,128)(2,1)S(1)} %broadcast_select_fusion), channel_id=1, source_target_pairs={{0,1},{1,2},{2,3},{3,0},{4,7},{5,4},{6,5},{7,6},{8,9},{9,10},{10,1... | collective-permute-start | bytes 1966088 | tf_op jit(solution)/shard_map/ppermute | solution.py:44
  36.3 12.8 %collective-permute-start = (bf16[512,640]{1,0:T(8,128)(2,1)}, bf16[512,640]{1,0:T(8,128)(2,1)}, u32[]{:S(2)}, u32[]{:S(2)}) collective-permute-start(bf16[512,640]{1,0:T(8,128)(2,1)} %refs_0_), channel_id=1, source_target_pairs={{0,4},{4,0},{1,5},{5,1},{2,6},{6,2},{3,7},{7,3},{8,12},{12,8},{9,1... | collective-permute-start | bytes 1966088 | tf_op jit(solution)/shard_map/ppermute | solution.py:37
  36.5 12.5 %collective-permute-start.2 = (bf16[512,640]{1,0:T(8,128)(2,1)S(1)}, bf16[512,640]{1,0:T(8,128)(2,1)}, u32[]{:S(2)}, u32[]{:S(2)}) collective-permute-start(bf16[512,640]{1,0:T(8,128)(2,1)S(1)} %collective-permute-done.1.refs_2_), channel_id=1, source_target_pairs={{0,4},{4,0},{1,5},{5,1},{2,6},{6,2},{3,7},{7,3},{8,12},{12,8},{9,1... | collective-permute-start | bytes 1966088 | tf_op jit(solution)/shard_map/ppermute | solution.py:37
  37.1 11.9 %collective-permute-start.6 = (bf16[512,640]{1,0:T(8,128)(2,1)}, bf16[512,640]{1,0:T(8,128)(2,1)}, u32[]{:S(2)}, u32[]{:S(2)}) collective-permute-start(bf16[512,640]{1,0:T(8,128)(2,1)} %collective-permute-done.3.refs_6_), channel_id=1, source_target_pairs={{0,4},{4,0},{1,5},{5,1},{2,6},{6,2},{3,7},{7,3},{8,12},{12,8},{9,1... | collective-permute-start | bytes 1966088 | tf_op jit(solution)/shard_map/ppermute | solution.py:37
  38.1 10.9 %collective-permute-start.9 = (bf16[3,160,640]{2,1,0:T(8,128)(2,1)}, bf16[3,160,640]{2,1,0:T(8,128)(2,1)}, u32[]{:S(2)}, u32[]{:S(2)}) collective-permute-start(bf16[3,160,640]{2,1,0:T(8,128)(2,1)} %broadcast_select_fusion.1), channel_id=1, source_target_pairs={{0,64},{64,128},{128,192},{192,0},{4,196},{68,4},{132,68},{196,132... | collective-permute-start | bytes 1843208 | tf_op jit(solution)/shard_map/ppermute | solution.py:45
  80.1 15.0 %collective-permute-start.15 = (bf16[680,384]{1,0:T(8,128)(2,1)S(1)}, bf16[680,384]{1,0:T(8,128)(2,1)S(1)}, u32[]{:S(2)}, u32[]{:S(2)}) collective-permute-start(bf16[680,384]{1,0:T(8,128)(2,1)S(1)} %fusion.25), channel_id=1, source_target_pairs={{0,64},{64,128},{128,192},{192,0},{4,196},{68,4},{132,68},{196,132... | collective-permute-start | bytes 1566728 | tf_op jit(solution)/shard_map/ppermute | solution.py:45
  80.7 12.2 %collective-permute-start.25 = (bf16[640,256]{1,0:T(8,128)(2,1)S(1)}, bf16[640,256]{1,0:T(8,128)(2,1)S(1)}, u32[]{:S(2)}, u32[]{:S(2)}) collective-permute-start(bf16[640,256]{1,0:T(8,128)(2,1)S(1)} %convolution_convert_fusion.1), channel_id=1, source_target_pairs={{0,64},{64,128},{128,192},{192,0},{4,196},{68,4},{132,68},{196,132... | collective-permute-start | bytes 983048 | tf_op jit(solution)/shard_map/ppermute | solution.py:45
  93.0 10.7 %collective-permute-start.26 = (bf16[640,256]{1,0:T(8,128)(2,1)S(1)}, bf16[640,256]{1,0:T(8,128)(2,1)S(1)}, u32[]{:S(2)}, u32[]{:S(2)}) collective-permute-start(bf16[640,256]{1,0:T(8,128)(2,1)S(1)} %get-tuple-element.56), channel_id=1, source_target_pairs={{0,64},{64,128},{128,192},{192,0},{1,65},{65,129},{129,193},{193,1... | collective-permute-start | bytes 983048 | tf_op jit(solution)/shard_map/ppermute | solution.py:33
  94.8 11.8 %collective-permute-start.27 = (bf16[640,256]{1,0:T(8,128)(2,1)S(1)}, bf16[640,256]{1,0:T(8,128)(2,1)S(1)}, u32[]{:S(2)}, u32[]{:S(2)}) collective-permute-start(bf16[640,256]{1,0:T(8,128)(2,1)S(1)} %get-tuple-element.57), channel_id=1, source_target_pairs={{0,192},{64,0},{128,64},{192,128},{1,193},{65,1},{129,65},{193,129... | collective-permute-start | bytes 983048 | tf_op jit(solution)/shard_map/ppermute | solution.py:33
  95.8 17.9 %collective-permute-start.17 = (bf16[680,384]{1,0:T(8,128)(2,1)S(1)}, bf16[680,384]{1,0:T(8,128)(2,1)S(1)}, u32[]{:S(2)}, u32[]{:S(2)}) collective-permute-start(bf16[680,384]{1,0:T(8,128)(2,1)S(1)} %fusion.27), channel_id=1, source_target_pairs={{0,192},{64,0},{128,64},{192,128},{1,193},{65,1},{129,65},{193,129... | collective-permute-start | bytes 1566728 | tf_op jit(solution)/shard_map/ppermute | solution.py:33
  96.7 17.0 %collective-permute-start.16 = (bf16[680,384]{1,0:T(8,128)(2,1)S(1)}, bf16[680,384]{1,0:T(8,128)(2,1)S(1)}, u32[]{:S(2)}, u32[]{:S(2)}) collective-permute-start(bf16[680,384]{1,0:T(8,128)(2,1)S(1)} %fusion.26), channel_id=1, source_target_pairs={{0,64},{64,128},{128,192},{192,0},{1,65},{65,129},{129,193},{193,1... | collective-permute-start | bytes 1566728 | tf_op jit(solution)/shard_map/ppermute | solution.py:33
  114.3 16.5 %collective-permute-start.18 = (bf16[104,384]{1,0:T(8,128)(2,1)S(1)}, bf16[104,384]{1,0:T(8,128)(2,1)S(1)}, u32[]{:S(2)}, u32[]{:S(2)}) collective-permute-start(bf16[104,384]{1,0:T(8,128)(2,1)S(1)} %get-tuple-element.127), channel_id=1, source_target_pairs={{0,32},{8,40},{16,48},{24,56},{32,0},{40,8},{48,16},{56,24},{1,33}... | collective-permute-start | bytes 239624 | tf_op jit(solution)/shard_map/ppermute | solution.py:33
  121.6 10.6 %collective-permute-start.19 = (bf16[104,384]{1,0:T(8,128)(2,1)S(1)}, bf16[104,384]{1,0:T(8,128)(2,1)S(1)}, u32[]{:S(2)}, u32[]{:S(2)}) collective-permute-start(bf16[104,384]{1,0:T(8,128)(2,1)S(1)} %get-tuple-element.128), channel_id=1, source_target_pairs={{0,24},{8,32},{16,40},{24,48},{32,56},{40,0},{48,8},{56,16},{1,25}... | collective-permute-start | bytes 239624 | tf_op jit(solution)/shard_map/ppermute | solution.py:33
  123.5 14.8 %collective-permute-start.20 = (bf16[104,384]{1,0:T(8,128)(2,1)S(1)}, bf16[104,384]{1,0:T(8,128)(2,1)S(1)}, u32[]{:S(2)}, u32[]{:S(2)}) collective-permute-start(bf16[104,384]{1,0:T(8,128)(2,1)S(1)} %get-tuple-element.129), channel_id=1, source_target_pairs={{0,40},{8,48},{16,56},{24,0},{32,8},{40,16},{48,24},{56,32},{1,41}... | collective-permute-start | bytes 239624 | tf_op jit(solution)/shard_map/ppermute | solution.py:33
  126.6 11.7 %collective-permute-start.21 = (bf16[104,384]{1,0:T(8,128)(2,1)S(1)}, bf16[104,384]{1,0:T(8,128)(2,1)S(1)}, u32[]{:S(2)}, u32[]{:S(2)}) collective-permute-start(bf16[104,384]{1,0:T(8,128)(2,1)S(1)} %get-tuple-element.130), channel_id=1, source_target_pairs={{0,16},{8,24},{16,32},{24,40},{32,48},{40,56},{48,0},{56,8},{1,17}... | collective-permute-start | bytes 239624 | tf_op jit(solution)/shard_map/ppermute | solution.py:33
  128.1 10.2 %collective-permute-start.22 = (bf16[104,384]{1,0:T(8,128)(2,1)S(1)}, bf16[104,384]{1,0:T(8,128)(2,1)S(1)}, u32[]{:S(2)}, u32[]{:S(2)}) collective-permute-start(bf16[104,384]{1,0:T(8,128)(2,1)S(1)} %get-tuple-element.131), channel_id=1, source_target_pairs={{0,48},{8,56},{16,0},{24,8},{32,16},{40,24},{48,32},{56,40},{1,49}... | collective-permute-start | bytes 239624 | tf_op jit(solution)/shard_map/ppermute | solution.py:33
  134.8 14.5 %all-to-all-start.1 = ((bf16[8,80,256]{2,1,0:T(8,128)(2,1)}), bf16[8,80,256]{2,1,0:T(8,128)(2,1)S(1)}, u32[]{:S(2)}, u32[]{:S(2)}) async-start(bf16[8,80,256]{2,1,0:T(8,128)(2,1)} %broadcast_select_fusion.2), calls=%async_computation.1 | async-start | bytes 655360 | tf_op jit(solution)/shard_map/all_to_all | solution.py:28
  149.4 10.3 %collective-permute-start.28 = (bf16[80,640]{1,0:T(8,128)(2,1)S(1)}, bf16[80,640]{1,0:T(8,128)(2,1)S(1)}, u32[]{:S(2)}, u32[]{:S(2)}) collective-permute-start(bf16[80,640]{1,0:T(8,128)(2,1)S(1)} %pad_maximum_fusion.10), channel_id=1, source_target_pairs={{0,0},{1,65},{2,130},{3,195},{4,56},{5,121},{6,186},{7,251},{8,8},... | collective-permute-start | bytes 307208 | tf_op jit(solution)/shard_map/ppermute | solution.py:360
  (15 other events, 103.6 us)

commit v3 on v2

--- a/solution.py
+++ b/solution.py
@@ -121,8 +121,8 @@
 
 def hidden_kernel(where, *refs):
     rows, refs = refs[: NC * NY], refs[NC * NY :]
-    out_proj, w_own, w_low, w_high, w_far, resid, pack, gh, hidden_out, sums, *refs = refs
-    turned, a, w, res, hidden, sem = refs
+    out_proj, w_own, w_low, w_high, w_far, resid, pack, gh, hidden, sums, *refs = refs
+    turned, a, w, res, sem = refs
     y, c, x = where[0], where[1], where[2]
     count, half = rows[0].shape
     part = w_own.shape[1]
@@ -179,11 +179,9 @@
     for copy in ready[early:]:
         copy.wait()
     out += turn(halves[1])
-    out.append(fetch(hidden.at[halves[0]], hidden_out.at[halves[0]]))
     multiply(count)
     for copy in out:
         copy.wait()
-    fetch(hidden.at[halves[1]], hidden_out.at[halves[1]]).wait()
 
 
 def hidden_and_sums(where, rows, out_proj, weights, resid, pack, gh):
@@ -199,13 +197,12 @@
             num_scalar_prefetch=1,
             grid=(1,),
             in_specs=[any_space] * (NC * NY + 7) + [full(gh.shape)],
-            out_specs=[any_space, full((2 * members, total)), any_space],
+            out_specs=[full((total, half)), full((2 * members, total)), any_space],
             scratch_shapes=[
                 pltpu.VMEM((total, NY * half), BF),
                 pltpu.VMEM((NY, half, half), BF),
                 pltpu.VMEM((total, half), BF),
-                pltpu.VMEM((total, half), F32),
-                pltpu.SemaphoreType.DMA((25,)),
+                pltpu.SemaphoreType.DMA((23,)),
             ],
         ),
         out_shape=[

time: 161 us -> 161 us (level)
  no operation moved by 1% of the time
where the time goes in v3:
time: 161 us
  waiting for transfers between devices  73.4 us (46%)
  starting transfers between devices  49.1 us (30%)
  Pallas kernels  11.3 us (7%)
  other arithmetic  10.6 us (7%)
  matrix products  10.5 us (7%)
  local copies, waits for them, and re-layouts  4.41 us (3%)
    ppermute x18, starting transfers between devices, shift(): return lax.ppermute(x, axis, [(i, (i + by) % n) for i in range(n)])  33.5 us
    ppermute x18, waiting for transfers between devices, shift(): return lax.ppermute(x, axis, [(i, (i + by) % n) for i in range(n)])  29.5 us
    all_to_all x2, waiting for transfers between devices, exchanged(): return lax.all_to_all(x, axis, split_axis=0, concat_axis=0, tiled=True)  18.6 us
    pallas_call x1, Pallas kernels, hidden_and_sums(): pl.pallas_call(hidden_kernel, grid_spec=pltpu.PrefetchScalarGridSpec(num_...  11.3 us
    ppermute x1, waiting for transfers between devices, shift_by_core(): lax.ppermute(x, ('c', axis), [(c * n + i, c * n + j) for c, i, j in moves])  9.15 us
    dot_general x5, matrix products, term(): return jnp.einsum('rd,rj->dj', left, right, preferred_element_type=F32)  9.07 us
    ppermute x3, waiting for transfers between devices, shift_by_core(): lax.ppermute(x, (axis, 'c'), [(i * NC + c, j * NC + c) for c, i, j in mov...  8.14 us
    all_to_all x2, starting transfers between devices, exchanged(): return lax.all_to_all(x, axis, split_axis=0, concat_axis=0, tiled=True)  8.03 us
  transfers between devices with their start and end apart: 32, of which 18 were waited for; matrix products, arithmetic and copies ran while one was open for 8% of the time, Pallas kernels for 0%

profile of v3, /device:TPU:6, one launch (start us, length us, event | category | flops | bytes accessed | tf_op | source)
XLA Modules:
  0.0 160.8 jit_solution(1992590285919448317)
XLA Ops:
  3.6 4.6 %all-to-all-start = ((bf16[4,160,640]{2,1,0:T(8,128)(2,1)}), bf16[4,160,640]{2,1,0:T(8,128)(2,1)S(1)}, u32[]{:S(2)}, u32[]{:S(2)}) async-start(bf16[4,160,640]{2,1,0:T(8,128)(2,1)} %pad_maximum_fusion), calls=%async_computation | async-start | bytes 1638400 | tf_op jit(solution)/shard_map/all_to_all | solution.py:28
  8.2 3.2 %collective-permute-start.1 = (bf16[512,640]{1,0:T(8,128)(2,1)}, bf16[512,640]{1,0:T(8,128)(2,1)S(1)}, u32[]{:S(2)}, u32[]{:S(2)}) collective-permute-start(bf16[512,640]{1,0:T(8,128)(2,1)} %refs_0_), channel_id=1, source_target_pairs={{0,3},{1,0},{2,1},{3,2},{4,7},{5,4},{6,5},{7,6},{8,11},{9,8},{10,9... | collective-permute-start | bytes 1966088 | tf_op jit(solution)/shard_map/ppermute | solution.py:33
  12.4 9.9 %all-to-all-done = bf16[4,160,640]{2,1,0:T(8,128)(2,1)S(1)} async-done(((bf16[4,160,640]{2,1,0:T(8,128)(2,1)}), bf16[4,160,640]{2,1,0:T(8,128)(2,1)S(1)}, u32[]{:S(2)}, u32[]{:S(2)}) %all-to-all-start) | async-done | bytes 819232 | tf_op jit(solution)/shard_map/all_to_all | solution.py:28
  24.5 8.8 %collective-permute-done.1.refs_2_ = bf16[512,640]{1,0:T(8,128)(2,1)S(1)} collective-permute-done((bf16[512,640]{1,0:T(8,128)(2,1)}, bf16[512,640]{1,0:T(8,128)(2,1)S(1)}, u32[]{:S(2)}, u32[]{:S(2)}) %collective-permute-start.1) | collective-permute-done | bytes 655392 | tf_op jit(solution)/shard_map/ppermute | solution.py:33
  38.6 9.1 %collective-permute-done.4.refs_4_ = bf16[512,640]{1,0:T(8,128)(2,1)} collective-permute-done((bf16[512,640]{1,0:T(8,128)(2,1)S(1)}, bf16[512,640]{1,0:T(8,128)(2,1)}, u32[]{:S(2)}, u32[]{:S(2)}) %collective-permute-start.4) | collective-permute-done | bytes 655392 | tf_op jit(solution)/shard_map/ppermute | solution.py:44
  50.2 11.3 %hidden_and_sums.1 = (f32[1024,640]{1,0:T(8,128)}, f32[16,1024]{1,0:T(8,128)S(1)}, bf16[4096,640]{1,0:T(8,128)(2,1)}) custom-call(s32[3]{0:T(128)S(1)} %pad_add_fusion.where, bf16[512,640]{1,0:T(8,128)(2,1)} %refs_0_, bf16[512,640]{1,0:T(8,128)(2,1)} %collective-permute-done.refs_1_, bf16[512,640]{1,0:T(8,128)(2,1)} %copy-done.2, ...), custom_call_target="tpu_custom_call" | custom-call | flops 3355443200 | bytes 20971520 | tf_op jit(solution)/shard_map/hidden_and_sums/pallas_call | solution.py:194
  63.0 3.2 %collective-permute-start.13 = (f32[16,1024]{1,0:T(8,128)S(1)}, f32[16,1024]{1,0:T(8,128)S(1)}, u32[]{:S(2)}, u32[]{:S(2)}) collective-permute-start(f32[16,1024]{1,0:T(8,128)S(1)} %maximum_add_fusion), channel_id=1, source_target_pairs={{0,3},{1,0},{2,1},{3,2},{4,7},{5,4},{6,5},{7,6},{8,11},{9,8},{10,9... | collective-permute-start | bytes 196616 | tf_op jit(solution)/shard_map/ppermute | solution.py:33
  69.0 2.9 %collective-permute-done.14 = f32[16,1024]{1,0:T(8,128)S(1)} collective-permute-done((f32[16,1024]{1,0:T(8,128)S(1)}, f32[16,1024]{1,0:T(8,128)S(1)}, u32[]{:S(2)}, u32[]{:S(2)}) %collective-permute-start.14) | collective-permute-done | bytes 65568 | tf_op jit(solution)/shard_map/ppermute | solution.py:33
  75.4 2.5 %fusion.1 = f32[640,640]{1,0:T(8,128)S(1)} fusion(bf16[1024,640]{1,0:T(8,128)(2,1)S(1)} %subtract_convert_fusion, bf16[4096,640]{1,0:T(8,128)(2,1)} %get-tuple-element.44), kind=kOutput, calls=%fused_computation.3 | convolution fusion | flops 838860800 | bytes 4259840 | tf_op jit(solution)/shard_map/rd,rj->dj/dot_general | solution.py:283
  78.0 2.5 %fusion.3 = f32[640,640]{1,0:T(8,128)S(1)} fusion(bf16[1024,640]{1,0:T(8,128)(2,1)S(1)} %subtract_convert_fusion, bf16[4096,640]{1,0:T(8,128)(2,1)} %get-tuple-element.44), kind=kOutput, calls=%fused_computation.5 | convolution fusion | flops 838860800 | bytes 4259840 | tf_op jit(solution)/shard_map/rd,rj->dj/dot_general | solution.py:283
  82.6 2.5 %fusion.5 = f32[640,640]{1,0:T(8,128)S(1)} fusion(bf16[1024,640]{1,0:T(8,128)(2,1)S(1)} %subtract_convert_fusion, bf16[4096,640]{1,0:T(8,128)(2,1)} %get-tuple-element.44), kind=kOutput, calls=%fused_computation.7 | convolution fusion | flops 838860800 | bytes 4259840 | tf_op jit(solution)/shard_map/rd,rj->dj/dot_general | solution.py:283
  85.1 8.1 %collective-permute-done.25 = bf16[640,256]{1,0:T(8,128)(2,1)S(1)} collective-permute-done((bf16[640,256]{1,0:T(8,128)(2,1)S(1)}, bf16[640,256]{1,0:T(8,128)(2,1)S(1)}, u32[]{:S(2)}, u32[]{:S(2)}) %collective-permute-start.25) | collective-permute-done | bytes 327712 | tf_op jit(solution)/shard_map/ppermute | solution.py:45
  97.1 2.4 %collective-permute-start.16 = (bf16[680,384]{1,0:T(8,128)(2,1)S(1)}, bf16[680,384]{1,0:T(8,128)(2,1)S(1)}, u32[]{:S(2)}, u32[]{:S(2)}) collective-permute-start(bf16[680,384]{1,0:T(8,128)(2,1)S(1)} %fusion.26), channel_id=1, source_target_pairs={{0,64},{64,128},{128,192},{192,0},{1,65},{65,129},{129,193},{193,1... | collective-permute-start | bytes 1566728 | tf_op jit(solution)/shard_map/ppermute | solution.py:33
  99.5 4.6 %collective-permute-done.26 = bf16[640,256]{1,0:T(8,128)(2,1)S(1)} collective-permute-done((bf16[640,256]{1,0:T(8,128)(2,1)S(1)}, bf16[640,256]{1,0:T(8,128)(2,1)S(1)}, u32[]{:S(2)}, u32[]{:S(2)}) %collective-permute-start.26) | collective-permute-done | bytes 327712 | tf_op jit(solution)/shard_map/ppermute | solution.py:33
  104.1 2.9 %collective-permute-done.27 = bf16[640,256]{1,0:T(8,128)(2,1)S(1)} collective-permute-done((bf16[640,256]{1,0:T(8,128)(2,1)S(1)}, bf16[640,256]{1,0:T(8,128)(2,1)S(1)}, u32[]{:S(2)}, u32[]{:S(2)}) %collective-permute-start.27) | collective-permute-done | bytes 327712 | tf_op jit(solution)/shard_map/ppermute | solution.py:33
  107.2 6.9 %collective-permute-done.17 = bf16[680,384]{1,0:T(8,128)(2,1)S(1)} collective-permute-done((bf16[680,384]{1,0:T(8,128)(2,1)S(1)}, bf16[680,384]{1,0:T(8,128)(2,1)S(1)}, u32[]{:S(2)}, u32[]{:S(2)}) %collective-permute-start.17) | collective-permute-done | bytes 522272 | tf_op jit(solution)/shard_map/ppermute | solution.py:33
  114.7 7.3 %collective-permute-start.18 = (bf16[104,384]{1,0:T(8,128)(2,1)S(1)}, bf16[104,384]{1,0:T(8,128)(2,1)S(1)}, u32[]{:S(2)}, u32[]{:S(2)}) collective-permute-start(bf16[104,384]{1,0:T(8,128)(2,1)S(1)} %get-tuple-element.127), channel_id=1, source_target_pairs={{0,32},{8,40},{16,48},{24,56},{32,0},{40,8},{48,16},{56,24},{1,33}... | collective-permute-start | bytes 239624 | tf_op jit(solution)/shard_map/ppermute | solution.py:33
  121.9 1.9 %collective-permute-start.19 = (bf16[104,384]{1,0:T(8,128)(2,1)S(1)}, bf16[104,384]{1,0:T(8,128)(2,1)S(1)}, u32[]{:S(2)}, u32[]{:S(2)}) collective-permute-start(bf16[104,384]{1,0:T(8,128)(2,1)S(1)} %get-tuple-element.128), channel_id=1, source_target_pairs={{0,24},{8,32},{16,40},{24,48},{32,56},{40,0},{48,8},{56,16},{1,25}... | collective-permute-start | bytes 239624 | tf_op jit(solution)/shard_map/ppermute | solution.py:33
  123.9 3.1 %collective-permute-start.20 = (bf16[104,384]{1,0:T(8,128)(2,1)S(1)}, bf16[104,384]{1,0:T(8,128)(2,1)S(1)}, u32[]{:S(2)}, u32[]{:S(2)}) collective-permute-start(bf16[104,384]{1,0:T(8,128)(2,1)S(1)} %get-tuple-element.129), channel_id=1, source_target_pairs={{0,40},{8,48},{16,56},{24,0},{32,8},{40,16},{48,24},{56,32},{1,41}... | collective-permute-start | bytes 239624 | tf_op jit(solution)/shard_map/ppermute | solution.py:33
  128.4 2.7 %collective-permute-start.22 = (bf16[104,384]{1,0:T(8,128)(2,1)S(1)}, bf16[104,384]{1,0:T(8,128)(2,1)S(1)}, u32[]{:S(2)}, u32[]{:S(2)}) collective-permute-start(bf16[104,384]{1,0:T(8,128)(2,1)S(1)} %get-tuple-element.131), channel_id=1, source_target_pairs={{0,48},{8,56},{16,0},{24,8},{32,16},{40,24},{48,32},{56,40},{1,49}... | collective-permute-start | bytes 239624 | tf_op jit(solution)/shard_map/ppermute | solution.py:33
  135.2 3.4 %all-to-all-start.1 = ((bf16[8,80,256]{2,1,0:T(8,128)(2,1)}), bf16[8,80,256]{2,1,0:T(8,128)(2,1)S(1)}, u32[]{:S(2)}, u32[]{:S(2)}) async-start(bf16[8,80,256]{2,1,0:T(8,128)(2,1)} %broadcast_select_fusion.2), calls=%async_computation.1 | async-start | bytes 655360 | tf_op jit(solution)/shard_map/all_to_all | solution.py:28
  141.0 8.7 %all-to-all-done.1 = bf16[8,80,256]{2,1,0:T(8,128)(2,1)S(1)} async-done(((bf16[8,80,256]{2,1,0:T(8,128)(2,1)}), bf16[8,80,256]{2,1,0:T(8,128)(2,1)S(1)}, u32[]{:S(2)}, u32[]{:S(2)}) %all-to-all-start.1) | async-done | bytes 327712 | tf_op jit(solution)/shard_map/all_to_all | solution.py:28
  149.8 3.6 %collective-permute-start.28 = (bf16[80,640]{1,0:T(8,128)(2,1)S(1)}, bf16[80,640]{1,0:T(8,128)(2,1)S(1)}, u32[]{:S(2)}, u32[]{:S(2)}) collective-permute-start(bf16[80,640]{1,0:T(8,128)(2,1)S(1)} %pad_maximum_fusion.10), channel_id=1, source_target_pairs={{0,0},{1,65},{2,130},{3,195},{4,56},{5,121},{6,186},{7,251},{8,8},... | collective-permute-start | bytes 307208 | tf_op jit(solution)/shard_map/ppermute | solution.py:357
  154.6 5.5 %collective-permute-done.28 = bf16[80,640]{1,0:T(8,128)(2,1)S(1)} collective-permute-done((bf16[80,640]{1,0:T(8,128)(2,1)S(1)}, bf16[80,640]{1,0:T(8,128)(2,1)S(1)}, u32[]{:S(2)}, u32[]{:S(2)}) %collective-permute-start.28) | collective-permute-done | bytes 102432 | tf_op jit(solution)/shard_map/ppermute | solution.py:357
  (153 shorter events, 37.5 us)
Async XLA Ops:
  3.6 18.7 %all-to-all-start = ((bf16[4,160,640]{2,1,0:T(8,128)(2,1)}), bf16[4,160,640]{2,1,0:T(8,128)(2,1)S(1)}, u32[]{:S(2)}, u32[]{:S(2)}) async-start(bf16[4,160,640]{2,1,0:T(8,128)(2,1)} %pad_maximum_fusion), calls=%async_computation | async-start | bytes 1638400 | tf_op jit(solution)/shard_map/all_to_all | solution.py:28
  8.2 25.2 %collective-permute-start.1 = (bf16[512,640]{1,0:T(8,128)(2,1)}, bf16[512,640]{1,0:T(8,128)(2,1)S(1)}, u32[]{:S(2)}, u32[]{:S(2)}) collective-permute-start(bf16[512,640]{1,0:T(8,128)(2,1)} %refs_0_), channel_id=1, source_target_pairs={{0,3},{1,0},{2,1},{3,2},{4,7},{5,4},{6,5},{7,6},{8,11},{9,8},{10,9... | collective-permute-start | bytes 1966088 | tf_op jit(solution)/shard_map/ppermute | solution.py:33
  11.4 23.2 %collective-permute-start.3 = (bf16[512,640]{1,0:T(8,128)(2,1)}, bf16[512,640]{1,0:T(8,128)(2,1)}, u32[]{:S(2)}, u32[]{:S(2)}) collective-permute-start(bf16[512,640]{1,0:T(8,128)(2,1)} %refs_0_), channel_id=1, source_target_pairs={{0,1},{1,2},{2,3},{3,0},{4,5},{5,6},{6,7},{7,4},{8,9},{9,10},{10,1... | collective-permute-start | bytes 1966088 | tf_op jit(solution)/shard_map/ppermute | solution.py:33
  12.4 25.7 %collective-permute-start.10 = (bf16[520,640]{1,0:T(8,128)(2,1)}, bf16[520,640]{1,0:T(8,128)(2,1)}, u32[]{:S(2)}, u32[]{:S(2)}) collective-permute-start(bf16[520,640]{1,0:T(8,128)(2,1)} %fusion.17), channel_id=1, source_target_pairs={{0,4},{4,0},{1,5},{5,1},{2,6},{6,2},{3,7},{7,3},{8,12},{12,8},{9,1... | collective-permute-start | bytes 1996808 | tf_op jit(solution)/shard_map/ppermute | solution.py:37
  22.4 14.1 %collective-permute-start.7 = (bf16[3,160,640]{2,1,0:T(8,128)(2,1)S(1)}, bf16[3,160,640]{2,1,0:T(8,128)(2,1)S(1)}, u32[]{:S(2)}, u32[]{:S(2)}) collective-permute-start(bf16[3,160,640]{2,1,0:T(8,128)(2,1)S(1)} %pad_maximum_fusion.1.refs_9_), channel_id=1, source_target_pairs={{0,64},{64,128},{128,192},{192,0},{1,65},{65,129},{129,193},{193,1... | collective-permute-start | bytes 1843208 | tf_op jit(solution)/shard_map/ppermute | solution.py:33
  23.7 13.4 %collective-permute-start.8 = (bf16[3,160,640]{2,1,0:T(8,128)(2,1)S(1)}, bf16[3,160,640]{2,1,0:T(8,128)(2,1)S(1)}, u32[]{:S(2)}, u32[]{:S(2)}) collective-permute-start(bf16[3,160,640]{2,1,0:T(8,128)(2,1)S(1)} %pad_maximum_fusion.1.refs_9_), channel_id=1, source_target_pairs={{0,192},{64,0},{128,64},{192,128},{1,193},{65,1},{129,65},{193,129... | collective-permute-start | bytes 1843208 | tf_op jit(solution)/shard_map/ppermute | solution.py:33
  35.8 12.0 %collective-permute-start.4 = (bf16[512,640]{1,0:T(8,128)(2,1)S(1)}, bf16[512,640]{1,0:T(8,128)(2,1)}, u32[]{:S(2)}, u32[]{:S(2)}) collective-permute-start(bf16[512,640]{1,0:T(8,128)(2,1)S(1)} %broadcast_select_fusion), channel_id=1, source_target_pairs={{0,1},{1,2},{2,3},{3,0},{4,7},{5,4},{6,5},{7,6},{8,9},{9,10},{10,1... | collective-permute-start | bytes 1966088 | tf_op jit(solution)/shard_map/ppermute | solution.py:44
  36.3 12.8 %collective-permute-start = (bf16[512,640]{1,0:T(8,128)(2,1)}, bf16[512,640]{1,0:T(8,128)(2,1)}, u32[]{:S(2)}, u32[]{:S(2)}) collective-permute-start(bf16[512,640]{1,0:T(8,128)(2,1)} %refs_0_), channel_id=1, source_target_pairs={{0,4},{4,0},{1,5},{5,1},{2,6},{6,2},{3,7},{7,3},{8,12},{12,8},{9,1... | collective-permute-start | bytes 1966088 | tf_op jit(solution)/shard_map/ppermute | solution.py:37
  36.5 12.5 %collective-permute-start.2 = (bf16[512,640]{1,0:T(8,128)(2,1)S(1)}, bf16[512,640]{1,0:T(8,128)(2,1)}, u32[]{:S(2)}, u32[]{:S(2)}) collective-permute-start(bf16[512,640]{1,0:T(8,128)(2,1)S(1)} %collective-permute-done.1.refs_2_), channel_id=1, source_target_pairs={{0,4},{4,0},{1,5},{5,1},{2,6},{6,2},{3,7},{7,3},{8,12},{12,8},{9,1... | collective-permute-start | bytes 1966088 | tf_op jit(solution)/shard_map/ppermute | solution.py:37
  37.1 11.9 %collective-permute-start.6 = (bf16[512,640]{1,0:T(8,128)(2,1)}, bf16[512,640]{1,0:T(8,128)(2,1)}, u32[]{:S(2)}, u32[]{:S(2)}) collective-permute-start(bf16[512,640]{1,0:T(8,128)(2,1)} %collective-permute-done.3.refs_6_), channel_id=1, source_target_pairs={{0,4},{4,0},{1,5},{5,1},{2,6},{6,2},{3,7},{7,3},{8,12},{12,8},{9,1... | collective-permute-start | bytes 1966088 | tf_op jit(solution)/shard_map/ppermute | solution.py:37
  38.1 10.9 %collective-permute-start.9 = (bf16[3,160,640]{2,1,0:T(8,128)(2,1)}, bf16[3,160,640]{2,1,0:T(8,128)(2,1)}, u32[]{:S(2)}, u32[]{:S(2)}) collective-permute-start(bf16[3,160,640]{2,1,0:T(8,128)(2,1)} %broadcast_select_fusion.1), channel_id=1, source_target_pairs={{0,64},{64,128},{128,192},{192,0},{4,196},{68,4},{132,68},{196,132... | collective-permute-start | bytes 1843208 | tf_op jit(solution)/shard_map/ppermute | solution.py:45
  80.5 15.0 %collective-permute-start.15 = (bf16[680,384]{1,0:T(8,128)(2,1)S(1)}, bf16[680,384]{1,0:T(8,128)(2,1)S(1)}, u32[]{:S(2)}, u32[]{:S(2)}) collective-permute-start(bf16[680,384]{1,0:T(8,128)(2,1)S(1)} %fusion.25), channel_id=1, source_target_pairs={{0,64},{64,128},{128,192},{192,0},{4,196},{68,4},{132,68},{196,132... | collective-permute-start | bytes 1566728 | tf_op jit(solution)/shard_map/ppermute | solution.py:45
  81.1 12.2 %collective-permute-start.25 = (bf16[640,256]{1,0:T(8,128)(2,1)S(1)}, bf16[640,256]{1,0:T(8,128)(2,1)S(1)}, u32[]{:S(2)}, u32[]{:S(2)}) collective-permute-start(bf16[640,256]{1,0:T(8,128)(2,1)S(1)} %convolution_convert_fusion.1), channel_id=1, source_target_pairs={{0,64},{64,128},{128,192},{192,0},{4,196},{68,4},{132,68},{196,132... | collective-permute-start | bytes 983048 | tf_op jit(solution)/shard_map/ppermute | solution.py:45
  93.4 10.7 %collective-permute-start.26 = (bf16[640,256]{1,0:T(8,128)(2,1)S(1)}, bf16[640,256]{1,0:T(8,128)(2,1)S(1)}, u32[]{:S(2)}, u32[]{:S(2)}) collective-permute-start(bf16[640,256]{1,0:T(8,128)(2,1)S(1)} %get-tuple-element.56), channel_id=1, source_target_pairs={{0,64},{64,128},{128,192},{192,0},{1,65},{65,129},{129,193},{193,1... | collective-permute-start | bytes 983048 | tf_op jit(solution)/shard_map/ppermute | solution.py:33
  95.2 11.8 %collective-permute-start.27 = (bf16[640,256]{1,0:T(8,128)(2,1)S(1)}, bf16[640,256]{1,0:T(8,128)(2,1)S(1)}, u32[]{:S(2)}, u32[]{:S(2)}) collective-permute-start(bf16[640,256]{1,0:T(8,128)(2,1)S(1)} %get-tuple-element.57), channel_id=1, source_target_pairs={{0,192},{64,0},{128,64},{192,128},{1,193},{65,1},{129,65},{193,129... | collective-permute-start | bytes 983048 | tf_op jit(solution)/shard_map/ppermute | solution.py:33
  96.2 17.9 %collective-permute-start.17 = (bf16[680,384]{1,0:T(8,128)(2,1)S(1)}, bf16[680,384]{1,0:T(8,128)(2,1)S(1)}, u32[]{:S(2)}, u32[]{:S(2)}) collective-permute-start(bf16[680,384]{1,0:T(8,128)(2,1)S(1)} %fusion.27), channel_id=1, source_target_pairs={{0,192},{64,0},{128,64},{192,128},{1,193},{65,1},{129,65},{193,129... | collective-permute-start | bytes 1566728 | tf_op jit(solution)/shard_map/ppermute | solution.py:33
  97.1 17.0 %collective-permute-start.16 = (bf16[680,384]{1,0:T(8,128)(2,1)S(1)}, bf16[680,384]{1,0:T(8,128)(2,1)S(1)}, u32[]{:S(2)}, u32[]{:S(2)}) collective-permute-start(bf16[680,384]{1,0:T(8,128)(2,1)S(1)} %fusion.26), channel_id=1, source_target_pairs={{0,64},{64,128},{128,192},{192,0},{1,65},{65,129},{129,193},{193,1... | collective-permute-start | bytes 1566728 | tf_op jit(solution)/shard_map/ppermute | solution.py:33
  114.7 16.5 %collective-permute-start.18 = (bf16[104,384]{1,0:T(8,128)(2,1)S(1)}, bf16[104,384]{1,0:T(8,128)(2,1)S(1)}, u32[]{:S(2)}, u32[]{:S(2)}) collective-permute-start(bf16[104,384]{1,0:T(8,128)(2,1)S(1)} %get-tuple-element.127), channel_id=1, source_target_pairs={{0,32},{8,40},{16,48},{24,56},{32,0},{40,8},{48,16},{56,24},{1,33}... | collective-permute-start | bytes 239624 | tf_op jit(solution)/shard_map/ppermute | solution.py:33
  121.9 10.6 %collective-permute-start.19 = (bf16[104,384]{1,0:T(8,128)(2,1)S(1)}, bf16[104,384]{1,0:T(8,128)(2,1)S(1)}, u32[]{:S(2)}, u32[]{:S(2)}) collective-permute-start(bf16[104,384]{1,0:T(8,128)(2,1)S(1)} %get-tuple-element.128), channel_id=1, source_target_pairs={{0,24},{8,32},{16,40},{24,48},{32,56},{40,0},{48,8},{56,16},{1,25}... | collective-permute-start | bytes 239624 | tf_op jit(solution)/shard_map/ppermute | solution.py:33
  123.9 14.8 %collective-permute-start.20 = (bf16[104,384]{1,0:T(8,128)(2,1)S(1)}, bf16[104,384]{1,0:T(8,128)(2,1)S(1)}, u32[]{:S(2)}, u32[]{:S(2)}) collective-permute-start(bf16[104,384]{1,0:T(8,128)(2,1)S(1)} %get-tuple-element.129), channel_id=1, source_target_pairs={{0,40},{8,48},{16,56},{24,0},{32,8},{40,16},{48,24},{56,32},{1,41}... | collective-permute-start | bytes 239624 | tf_op jit(solution)/shard_map/ppermute | solution.py:33
  127.0 11.7 %collective-permute-start.21 = (bf16[104,384]{1,0:T(8,128)(2,1)S(1)}, bf16[104,384]{1,0:T(8,128)(2,1)S(1)}, u32[]{:S(2)}, u32[]{:S(2)}) collective-permute-start(bf16[104,384]{1,0:T(8,128)(2,1)S(1)} %get-tuple-element.130), channel_id=1, source_target_pairs={{0,16},{8,24},{16,32},{24,40},{32,48},{40,56},{48,0},{56,8},{1,17}... | collective-permute-start | bytes 239624 | tf_op jit(solution)/shard_map/ppermute | solution.py:33
  128.4 10.2 %collective-permute-start.22 = (bf16[104,384]{1,0:T(8,128)(2,1)S(1)}, bf16[104,384]{1,0:T(8,128)(2,1)S(1)}, u32[]{:S(2)}, u32[]{:S(2)}) collective-permute-start(bf16[104,384]{1,0:T(8,128)(2,1)S(1)} %get-tuple-element.131), channel_id=1, source_target_pairs={{0,48},{8,56},{16,0},{24,8},{32,16},{40,24},{48,32},{56,40},{1,49}... | collective-permute-start | bytes 239624 | tf_op jit(solution)/shard_map/ppermute | solution.py:33
  135.2 14.5 %all-to-all-start.1 = ((bf16[8,80,256]{2,1,0:T(8,128)(2,1)}), bf16[8,80,256]{2,1,0:T(8,128)(2,1)S(1)}, u32[]{:S(2)}, u32[]{:S(2)}) async-start(bf16[8,80,256]{2,1,0:T(8,128)(2,1)} %broadcast_select_fusion.2), calls=%async_computation.1 | async-start | bytes 655360 | tf_op jit(solution)/shard_map/all_to_all | solution.py:28
  149.8 10.3 %collective-permute-start.28 = (bf16[80,640]{1,0:T(8,128)(2,1)S(1)}, bf16[80,640]{1,0:T(8,128)(2,1)S(1)}, u32[]{:S(2)}, u32[]{:S(2)}) collective-permute-start(bf16[80,640]{1,0:T(8,128)(2,1)S(1)} %pad_maximum_fusion.10), channel_id=1, source_target_pairs={{0,0},{1,65},{2,130},{3,195},{4,56},{5,121},{6,186},{7,251},{8,8},... | collective-permute-start | bytes 307208 | tf_op jit(solution)/shard_map/ppermute | solution.py:357
  (15 other events, 103.6 us)
